TPU v7x, 32 devices: a whole 2x2x4 slice. The times are simulated.
32 devices in a mesh: groups: 2 (over y), row: 4 (over z), col: 2 (over x), mp: 2 (over core).
Axes of the slice: x: 2, y: 2, z: 4, core: 2. Of those that a mesh axis runs over, the one named last changes fastest.
Arguments:
- queries: bfloat16 [2, 2048, 5120], P('mp', ('groups', 'row'), 'col'), parts along dimension 1, may hold values from -6 to 6
- keys: bfloat16 [2, 2048, 1024], P('mp', ('groups', 'row'), 'col'), parts along dimension 1, may hold values from -6 to 6
- values: bfloat16 [2, 2048, 1024], P('mp', ('groups', 'row'), 'col'), parts along dimension 1, may hold values from -6 to 6
- lengths: int32 [4], P('groups'), parts along dimension 0, may hold values from 1 to 768, 1024 in all
Outputs:
- outputs: bfloat16 [2, 2048, 5120], P('mp', ('groups', 'row'), 'col'), parts along dimension 1
- gap: float32 [40, 2048], P(('col', 'mp'), ('groups', 'row')), parts along dimension 1
There are 2 independent parts, one for each index of `groups`. A program takes and returns all parts, laid end to end along the dimension named above; each array names one. Nothing has to cross between parts.
Inputs may be any that keep to these rules, and one draw needn't show every extreme that they name: The 2 lengths sum to 1024; one rollout is exactly 768 tokens long.
All inputs are finite; a program needn't handle non-finite values.
Results may differ from a plain program's by a relative error of at most 0.011.
Values may be sent and summed in bfloat16 or wider, within the bound.
No kernel may reach another device: no remote copies, remote signals or barrier semaphores. Data moves between devices by JAX's collectives and lax.ppermute only.
A program may use at most 64 MiB of HBM per device.

v0:
```python
import math

import jax
import jax.numpy as jnp
from jax import lax
from jax.sharding import PartitionSpec as P

HEADS = 40
KV_HEADS = 8
HEAD_DIM = 128


def from_behind(block, axis, distance):
    devices = range(lax.axis_size(axis))
    route = [(i - distance, i) for i in devices if i - distance in devices]
    return lax.ppermute(block, axis, route)


def swapped(block, axis, distance):
    count = lax.axis_size(axis)
    route = []
    for low in range(count):
        high = low | 1 << distance
        if high != low and high < count:
            route += [(low, high), (high, low)]
    return lax.ppermute(block, axis, route)


def relative_gap(first, second, tokens_here, heads_count):
    first = first.astype(jnp.float32).reshape(tokens_here, heads_count, HEAD_DIM)
    second = second.astype(jnp.float32).reshape(tokens_here, heads_count, HEAD_DIM)
    difference = first - second
    scale_sum = jnp.mean(first * first, axis=-1) + 1e-06
    return jnp.transpose(jnp.mean(difference * difference, axis=-1) / scale_sum)


def per_device(queries, keys, values, lengths):
    tokens_here = queries.shape[1]
    width_here = keys.shape[2]
    kv_local = width_here // HEAD_DIM
    group_size = HEADS // KV_HEADS
    heads_local = kv_local * group_size
    factor = 1.0 / math.sqrt(HEAD_DIM)
    row_pos = lax.axis_index("row")
    first_pos = row_pos * tokens_here
    query_pos = first_pos + jnp.arange(tokens_here, dtype=jnp.int32)
    finish = jnp.cumsum(lengths)
    begin_at = jnp.sum(
        jnp.where(finish[None, :] <= query_pos[:, None], lengths[None, :], 0), axis=1
    )
    lowest = begin_at[0]
    highest = first_pos + tokens_here - 1
    query_rows = queries[0].reshape(tokens_here, kv_local, group_size, HEAD_DIM)

    def update(running, stacked, offset):
        best, summed, accum = running
        amount = stacked.shape[1]
        key_rows = stacked[0].reshape(amount, kv_local, HEAD_DIM)
        value_rows = stacked[1].reshape(amount, kv_local, HEAD_DIM)
        scores = (
            jnp.einsum("tkgd,nkd->kgtn", query_rows, key_rows, preferred_element_type=jnp.float32)
            * factor
        )
        key_pos = offset + jnp.arange(amount, dtype=jnp.int32)
        allowed = (key_pos[None, :] >= begin_at[:, None]) & (key_pos[None, :] <= query_pos[:, None])
        masked = jnp.where(allowed, scores, -jnp.inf)
        fresh_best = jnp.maximum(best, jnp.max(masked, axis=-1))
        weights = jnp.where(allowed, jnp.exp(masked - fresh_best[..., None]), 0.0)
        shrink = jnp.exp(best - fresh_best)
        summed = summed * shrink + jnp.sum(weights, axis=-1)
        accum = accum * shrink[..., None] + jnp.einsum(
            "kgtn,nkd->kgtd",
            weights.astype(jnp.bfloat16),
            value_rows,
            preferred_element_type=jnp.float32,
        )
        return (fresh_best, summed, accum)

    def absorb(running, stacked, offset):
        amount = stacked.shape[1]
        needed = (offset + amount > lowest) & (offset <= highest)
        return lax.cond(
            needed, lambda inner: update(inner, stacked, offset), lambda inner: inner, running
        )

    start_state = (
        jnp.full((kv_local, group_size, tokens_here), -1e30, jnp.float32),
        jnp.zeros((kv_local, group_size, tokens_here), jnp.float32),
        jnp.zeros((kv_local, group_size, tokens_here, HEAD_DIM), jnp.float32),
    )
    paired = jnp.concatenate([keys, values], axis=0)
    reach = lax.axis_size("row") // 2 + 1
    running = absorb(start_state, paired, first_pos)

    def advance(step_id, loop_state):
        inner, moving = loop_state
        moving = from_behind(moving, "row", 1)
        return (absorb(inner, moving, (row_pos - step_id) * tokens_here), moving)

    running, _ = lax.fori_loop(1, reach + 1, advance, (running, paired))
    best, summed, accum = running
    mixed = accum / summed[..., None]
    outputs = (
        jnp.transpose(mixed, (2, 0, 1, 3))
        .reshape(tokens_here, heads_local * HEAD_DIM)
        .astype(jnp.bfloat16)[None]
    )
    half_heads = heads_local // 2
    partner = swapped(outputs, "mp", 0)
    model_pos = lax.axis_index("mp")
    is_policy = model_pos == 0
    policy = jnp.where(is_policy, outputs[0], partner[0])
    anchor = jnp.where(is_policy, partner[0], outputs[0])
    column_at = model_pos * half_heads * HEAD_DIM
    policy_part = lax.dynamic_slice_in_dim(policy, column_at, half_heads * HEAD_DIM, 1)
    anchor_part = lax.dynamic_slice_in_dim(anchor, column_at, half_heads * HEAD_DIM, 1)
    gap = relative_gap(policy_part, anchor_part, tokens_here, half_heads)
    return (outputs, gap)


def solution(mesh):
    in_specs = (
        P("mp", ("groups", "row"), "col"),
        P("mp", ("groups", "row"), "col"),
        P("mp", ("groups", "row"), "col"),
        P("groups"),
    )
    out_specs = (P("mp", ("groups", "row"), "col"), P(("col", "mp"), ("groups", "row")))
    return jax.shard_map(
        per_device, mesh=mesh, in_specs=in_specs, out_specs=out_specs, check_vma=False
    )
```

profile of v0, /device:TPU:17, one launch (start us, length us, event | category | flops | bytes accessed | tf_op | source)
XLA Modules:
  0.0 102.2 jit_solution(17828449757495927564)
XLA Ops:
  0.7 0.9 reduce-window.8
  2.9 1.6 %copy.31 = bf16[1,256,2560]{1,2,0:T(8,128)(2,1)S(1)} copy(bf16[1,256,2560]{2,1,0:T(8,128)(2,1)} %param.10) | data formatting | bytes 2621440 | tf_op args[0]
  4.5 1.1 %copy.34 = bf16[1,256,512]{1,2,0:T(8,128)(2,1)S(1)} copy(bf16[1,256,512]{2,1,0:T(8,128)(2,1)} %param.12) | data formatting | bytes 524288 | tf_op args[2]
  5.6 1.8 %copy.33 = bf16[1,256,512]{1,2,0:T(8,128)(2,1)} copy(bf16[1,256,512]{2,1,0:T(8,128)(2,1)} %param.11) | data formatting | bytes 524288 | tf_op args[1]
  8.8 1.8 %pad_maximum_fusion = bf16[2,256,512]{1,2,0:T(8,128)(2,1)} fusion(bf16[1,256,512]{1,2,0:T(8,128)(2,1)S(1)} %copy.34, bf16[1,256,512]{1,2,0:T(8,128)(2,1)} %copy.33), kind=kLoop, calls=%fused_computation.49 | loop fusion | flops 262144 | bytes 1048576 | tf_op jit(solution)/shard_map/concatenate | solution.py:91
  10.6 12.4 %conditional.2 = (f32[4,5,256]{2,1,0:T(8,128)}, f32[4,5,256]{2,1,0:T(8,128)S(1)}, f32[4,5,256,128]{3,2,1,0:T(8,128)}) conditional(s32[]{:T(128)} %convert_element_type.42, () %tuple.37, (s32[]{:T(128)}, s32[256]{0:T(256)S(1)}, s32[256]{0:T(256)S(1)}, bf16[1,256,512]{2,1,0:T(8,128)(2,1)S(1)}, bf16[256,4,5,128]{0,3,2,1:T(8,128)(2,1)S(1)}, ...), branch_computations={%region_2.3_spmd, %region_3.6_spmd} | conditional | flops 689000704 | bytes 42696760 | solution.py:82
  10.8 0.9 fusion.2
  12.4 1.7 %copy-done = f32[4,256,256,5]{2,1,3,0:T(8,128)} copy-done((f32[4,256,256,5]{2,1,3,0:T(8,128)}, f32[4,256,256,5]{2,1,3,0:T(8,128)S(1)}, u32[]{:S(2)}) %copy-start) | copy-done | bytes 5242904 | tf_op jit(solution)/shard_map/cond
  14.1 2.0 %fusion.4 = f32[4,5,256]{2,1,0:T(8,128)S(1)} fusion(f32[4,256,256,5]{2,1,3,0:T(8,128)S(1)} %get-tuple-element.348, f32[4,5,256]{2,1,0:T(8,128)} %get-tuple-element.439, pred[256,256]{0,1:T(8,128)(4,1)S(1)} %compare_and_fusion), kind=kLoop, calls=%fused_computation.5 | loop fusion | flops 6548480 | bytes 5349376 | tf_op jit(solution)/shard_map/cond/branch_1_fun/reduce_sum | solution.py:70
  16.9 6.1 %fusion.12 = f32[4,5,256,128]{3,2,1,0:T(8,128)} fusion(f32[4,256,256,5]{2,1,3,0:T(8,128)} %copy-done, f32[4,5,256]{2,1,0:T(8,128)} %get-tuple-element.439, pred[256,256]{0,1:T(8,128)(4,1)S(1)} %compare_and_fusion, f32[4,5,256]{2,1,0:T(8,128)S(1)} %get-tuple-element.343, bf16[256,4,128,1]{2,1,0,3:T(4,128)(2,1)S(1)} %bitcast.67), kind=kOutput, calls=%fused_computation.12 | convolution fusion | flops 342753280 | bytes 8232960 | tf_op jit(solution)/shard_map/cond/branch_1_fun/kgtn,nkd->kgtd/dot_general | solution.py:71
  23.1 62.2 %while.20 = (s32[]{:T(128)}, f32[4,5,256]{2,1,0:T(8,128)}, f32[4,5,256]{2,1,0:T(8,128)S(1)}, f32[4,5,256,128]{3,2,1,0:T(8,128)}, bf16[2,256,512]{1,2,0:T(8,128)(...) while((s32[]{:T(128)}, f32[4,5,256]{2,1,0:T(8,128)}, ...), condition=%wide.region_11.12_spmd.clone, body=%wide.region_6.11_spmd.clone.sunk | while | flops 689646080 | bytes 27598188 | solution.py:100
  23.1 3.2 %collective-permute-start = (bf16[2,256,512]{1,2,0:T(8,128)(2,1)}, bf16[2,256,512]{1,2,0:T(8,128)(2,1)S(1)}, u32[]{:S(2)}, u32[]{:S(2)}) collective-permute-start(bf16[2,256,512]{1,2,0:T(8,128)(2,1)} %get-tuple-element.459), channel_id=1, source_target_pairs={{0,4},{4,8},{8,12},{1,5},{5,9},{9,13},{2,6},{6,10},{10,14},{3,7},{... | collective-permute-start | bytes 1572872 | tf_op jit(solution)/shard_map/while/body/eval_jaxpr/ppermute | solution.py:16
  26.9 11.0 %collective-permute-done = bf16[2,256,512]{1,2,0:T(8,128)(2,1)S(1)} collective-permute-done((bf16[2,256,512]{1,2,0:T(8,128)(2,1)}, bf16[2,256,512]{1,2,0:T(8,128)(2,1)S(1)}, u32[]{:S(2)}, u32[]{:S(2)}) %collective-permute-start) | collective-permute-done | bytes 524320 | tf_op jit(solution)/shard_map/while/body/eval_jaxpr/ppermute | solution.py:16
  38.0 9.3 %conditional.5 = ((f32[4,5,256]{2,1,0:T(8,128)}, f32[4,5,256]{2,1,0:T(8,128)S(1)}, f32[4,5,256,128]{3,2,1,0:T(8,128)})) conditional(s32[]{:T(128)} %convert_element_type.65, (f32[4,5,256]{2,1,0:T(8,128)}, f32[4,5,256]{2,1,0:T(8,128)S(1)}, f32[4,5,256,128]{3,2,1,0:T(8,128)}) %tuple.69, (s32[]{:T(128)}, s32[256]{0:T(256)S(1)}, s32[]{:T(128)}, ...), branch_computations={%region_7.7_spmd, %region_8.10_spmd} | conditional | flops 689646080 | bytes 24451112 | solution.py:82
  38.2 1.0 %fusion.22 = (f32[4,5,256]{2,1,0:T(8,128)S(1)}, f32[4,256,256,5]{2,1,3,0:T(8,128)S(1)}) fusion(pred[256,256]{0,1:T(8,128)(4,1)S(1)} %compare_and_fusion.1, bf16[256,4,128,1]{0,2,3,1:T(8,128)(2,1)S(1)} %bitcast.56, bf16[256,4,5,128]{3,0,2,1:T(8,128)(2,1)S(1)} %get-tuple-element.222), kind=kOutput, calls=%fused_computation.26 | convolution fusion | flops 339471360 | bytes 6901760 | tf_op jit(solution)/shard_map/while/body/eval_jaxpr/cond/branch_1_fun/tkgd,nkd->kgtn/dot_general | solution.py:61
  40.0 1.3 %fusion.24 = f32[4,5,256]{2,1,0:T(8,128)S(1)} fusion(f32[4,256,256,5]{2,1,3,0:T(8,128)S(1)} %get-tuple-element.352, f32[4,5,256]{2,1,0:T(8,128)S(1)} %max.2, pred[256,256]{0,1:T(8,128)(4,1)S(1)} %compare_and_fusion.1), kind=kLoop, calls=%fused_computation.28 | loop fusion | flops 6548480 | bytes 5349376 | tf_op jit(solution)/shard_map/while/body/eval_jaxpr/cond/branch_1_fun/reduce_sum | solution.py:70
  42.6 4.7 %multiply_add_fusion = f32[4,5,256,128]{3,2,1,0:T(8,128)} fusion(f32[4,5,256,128]{3,2,1,0:T(8,128)} %get-tuple-element.224, bf16[256,4,128,1]{0,2,3,1:T(8,128)(2,1)S(1)} %bitcast.62, f32[4,256,256,5]{2,1,3,0:T(8,128)S(1)} %get-tuple-element.352, f32[4,5,256]{2,1,0:T(8,128)S(1)} %max.2, pred[256,256]{0,1:T(8,128)(4,1)S(1)} %compare_and_fusion.1, ...), kind=kOutput, calls=%fused_computation.30 | convolution fusion | flops 343408640 | bytes 10854400 | tf_op jit(solution)/shard_map/while/body/eval_jaxpr/cond/branch_1_fun/kgtn,nkd->kgtd/dot_general | solution.py:71
  47.3 0.8 copy.85
  48.1 3.1 %collective-permute-start = (bf16[2,256,512]{1,2,0:T(8,128)(2,1)}, bf16[2,256,512]{1,2,0:T(8,128)(2,1)S(1)}, u32[]{:S(2)}, u32[]{:S(2)}) collective-permute-start(bf16[2,256,512]{1,2,0:T(8,128)(2,1)} %get-tuple-element.459), channel_id=1, source_target_pairs={{0,4},{4,8},{8,12},{1,5},{5,9},{9,13},{2,6},{6,10},{10,14},{3,7},{... | collective-permute-start | bytes 1572872 | tf_op jit(solution)/shard_map/while/body/eval_jaxpr/ppermute | solution.py:16
  51.9 10.2 %collective-permute-done = bf16[2,256,512]{1,2,0:T(8,128)(2,1)S(1)} collective-permute-done((bf16[2,256,512]{1,2,0:T(8,128)(2,1)}, bf16[2,256,512]{1,2,0:T(8,128)(2,1)S(1)}, u32[]{:S(2)}, u32[]{:S(2)}) %collective-permute-start) | collective-permute-done | bytes 524320 | tf_op jit(solution)/shard_map/while/body/eval_jaxpr/ppermute | solution.py:16
  62.1 0.8 copy.85
  62.9 12.4 %collective-permute-start = (bf16[2,256,512]{1,2,0:T(8,128)(2,1)}, bf16[2,256,512]{1,2,0:T(8,128)(2,1)S(1)}, u32[]{:S(2)}, u32[]{:S(2)}) collective-permute-start(bf16[2,256,512]{1,2,0:T(8,128)(2,1)} %get-tuple-element.459), channel_id=1, source_target_pairs={{0,4},{4,8},{8,12},{1,5},{5,9},{9,13},{2,6},{6,10},{10,14},{3,7},{... | collective-permute-start | bytes 1572872 | tf_op jit(solution)/shard_map/while/body/eval_jaxpr/ppermute | solution.py:16
  76.0 8.5 %collective-permute-done = bf16[2,256,512]{1,2,0:T(8,128)(2,1)S(1)} collective-permute-done((bf16[2,256,512]{1,2,0:T(8,128)(2,1)}, bf16[2,256,512]{1,2,0:T(8,128)(2,1)S(1)}, u32[]{:S(2)}, u32[]{:S(2)}) %collective-permute-start) | collective-permute-done | bytes 524320 | tf_op jit(solution)/shard_map/while/body/eval_jaxpr/ppermute | solution.py:16
  84.5 0.8 copy.85
  85.3 3.2 %copy.36 = f32[4,5,256,128]{2,3,1,0:T(8,128)} copy(f32[4,5,256,128]{3,2,1,0:T(8,128)} %get-tuple-element.250) | data formatting | bytes 5242880 | tf_op jit(solution)/shard_map/while | solution.py:100
  88.5 2.0 %divide_convert_fusion = bf16[4,5,256,128]{2,3,1,0:T(8,128)(2,1)S(1)} fusion(f32[4,5,256,128]{2,3,1,0:T(8,128)} %copy.36, f32[4,5,256]{2,1,0:T(8,128)S(1)} %get-tuple-element.251), kind=kLoop, calls=%fused_computation.44 | loop fusion | flops 1310720 | bytes 3952640 | tf_op jit(solution)/shard_map/convert_element_type | solution.py:106
  90.5 3.3 %collective-permute-start.1 = (bf16[1,256,2560]{1,2,0:T(8,128)(2,1)S(1)}, bf16[1,256,2560]{1,2,0:T(8,128)(2,1)S(1)}, u32[]{:S(2)}, u32[]{:S(2)}) collective-permute-start(bf16[1,256,2560]{1,2,0:T(8,128)(2,1)S(1)} %bitcast.59), channel_id=1, source_target_pairs={{0,1},{1,0},{2,3},{3,2},{4,5},{5,4},{6,7},{7,6},{8,9},{9,8},{10,11... | collective-permute-start | bytes 3932168 | tf_op jit(solution)/shard_map/ppermute | solution.py:26
  93.9 1.6 %copy.37 = bf16[1,256,2560]{2,1,0:T(8,128)(2,1)} copy(bf16[1,256,2560]{1,2,0:T(8,128)(2,1)S(1)} %bitcast.60) | data formatting | bytes 2621440
  95.4 1.1 %collective-permute-done.1 = bf16[1,256,2560]{1,2,0:T(8,128)(2,1)S(1)} collective-permute-done((bf16[1,256,2560]{1,2,0:T(8,128)(2,1)S(1)}, bf16[1,256,2560]{1,2,0:T(8,128)(2,1)S(1)}, u32[]{:S(2)}, u32[]{:S(2)}) %collective-permute-start.1) | collective-permute-done | bytes 1310752 | tf_op jit(solution)/shard_map/ppermute | solution.py:26
  96.5 1.1 %copy-done.3 = bf16[1,256,2560]{1,2,0:T(8,128)(2,1)} copy-done((bf16[1,256,2560]{1,2,0:T(8,128)(2,1)}, bf16[1,256,2560]{1,2,0:T(8,128)(2,1)S(1)}, u32[]{:S(2)}) %copy-start.3) | copy-done | bytes 1310744
  97.6 2.5 %fusion.37 = (f32[256,1280]{0,1:T(8,128)S(1)}, f32[256,1280]{0,1:T(8,128)}) fusion(pred[]{:T(512)S(6)} %eq.3, bf16[256,2560]{0,1:T(8,128)(2,1)} %bitcast.66, s32[]{:T(128)S(6)} %select_n.36, bf16[256,2560]{0,1:T(8,128)(2,1)S(1)} %bitcast.61), kind=kLoop, calls=%fused_computation.47 | loop fusion | flops 2293760 | bytes 3932165 | tf_op jit(solution)/shard_map/mul | solution.py:34
  100.1 1.4 %reduce_sum.47 = f32[256,10]{0,1:T(8,128)S(1)} reduce(f32[256,10,128]{0,2,1:T(8,128)} %bitcast.64, f32[]{:T(128)} %constant.68.clone.1), dimensions={2}, to_apply=%region_13.14 | reduce | flops 325120 | bytes 1320964 | tf_op jit(solution)/shard_map/reduce_sum | solution.py:33
  (29 shorter events, 6.8 us)
Async XLA Ops:
  0.6 8.2 %copy-start.2 = (bf16[1,256,512]{2,1,0:T(8,128)(2,1)S(1)}, bf16[1,256,512]{2,1,0:T(8,128)(2,1)}, u32[]{:S(2)}) copy-start(bf16[1,256,512]{2,1,0:T(8,128)(2,1)} %param.12) | copy-start | bytes 786436
  0.6 8.2 %copy-start.1 = (bf16[1,256,512]{2,1,0:T(8,128)(2,1)S(1)}, bf16[1,256,512]{2,1,0:T(8,128)(2,1)}, u32[]{:S(2)}) copy-start(bf16[1,256,512]{2,1,0:T(8,128)(2,1)} %param.11) | copy-start | bytes 786436
  11.7 2.3 %copy-start = (f32[4,256,256,5]{2,1,3,0:T(8,128)}, f32[4,256,256,5]{2,1,3,0:T(8,128)S(1)}, u32[]{:S(2)}) copy-start(f32[4,256,256,5]{2,1,3,0:T(8,128)S(1)} %get-tuple-element.348) | copy-start | bytes 15728644 | tf_op jit(solution)/shard_map/cond
  23.1 14.9 %collective-permute-start = (bf16[2,256,512]{1,2,0:T(8,128)(2,1)}, bf16[2,256,512]{1,2,0:T(8,128)(2,1)S(1)}, u32[]{:S(2)}, u32[]{:S(2)}) collective-permute-start(bf16[2,256,512]{1,2,0:T(8,128)(2,1)} %get-tuple-element.459), channel_id=1, source_target_pairs={{0,4},{4,8},{8,12},{1,5},{5,9},{9,13},{2,6},{6,10},{10,14},{3,7},{... | collective-permute-start | bytes 1572872 | tf_op jit(solution)/shard_map/while/body/eval_jaxpr/ppermute | solution.py:16
  48.1 14.1 %collective-permute-start = (bf16[2,256,512]{1,2,0:T(8,128)(2,1)}, bf16[2,256,512]{1,2,0:T(8,128)(2,1)S(1)}, u32[]{:S(2)}, u32[]{:S(2)}) collective-permute-start(bf16[2,256,512]{1,2,0:T(8,128)(2,1)} %get-tuple-element.459), channel_id=1, source_target_pairs={{0,4},{4,8},{8,12},{1,5},{5,9},{9,13},{2,6},{6,10},{10,14},{3,7},{... | collective-permute-start | bytes 1572872 | tf_op jit(solution)/shard_map/while/body/eval_jaxpr/ppermute | solution.py:16
  62.9 21.6 %collective-permute-start = (bf16[2,256,512]{1,2,0:T(8,128)(2,1)}, bf16[2,256,512]{1,2,0:T(8,128)(2,1)S(1)}, u32[]{:S(2)}, u32[]{:S(2)}) collective-permute-start(bf16[2,256,512]{1,2,0:T(8,128)(2,1)} %get-tuple-element.459), channel_id=1, source_target_pairs={{0,4},{4,8},{8,12},{1,5},{5,9},{9,13},{2,6},{6,10},{10,14},{3,7},{... | collective-permute-start | bytes 1572872 | tf_op jit(solution)/shard_map/while/body/eval_jaxpr/ppermute | solution.py:16
  90.5 6.0 %collective-permute-start.1 = (bf16[1,256,2560]{1,2,0:T(8,128)(2,1)S(1)}, bf16[1,256,2560]{1,2,0:T(8,128)(2,1)S(1)}, u32[]{:S(2)}, u32[]{:S(2)}) collective-permute-start(bf16[1,256,2560]{1,2,0:T(8,128)(2,1)S(1)} %bitcast.59), channel_id=1, source_target_pairs={{0,1},{1,0},{2,3},{3,2},{4,5},{5,4},{6,7},{7,6},{8,9},{9,8},{10,11... | collective-permute-start | bytes 3932168 | tf_op jit(solution)/shard_map/ppermute | solution.py:26
  96.5 1.1 %copy-start.3 = (bf16[1,256,2560]{1,2,0:T(8,128)(2,1)}, bf16[1,256,2560]{1,2,0:T(8,128)(2,1)S(1)}, u32[]{:S(2)}) copy-start(bf16[1,256,2560]{1,2,0:T(8,128)(2,1)S(1)} %collective-permute-done.1) | copy-start | bytes 3932164
where the time goes:
time: 104 us; the launch traced here: 102 us
  waiting for transfers between devices  30.8 us (30%)
  starting transfers between devices  22 us (21%)
  local copies, waits for them, and re-layouts  16.5 us (16%)
  other arithmetic  16.5 us (16%)
  matrix products  12.7 us (12%)
  loops' own time  2.19 us (2%)
  between operations  1.41 us (1%)
    ppermute x3, waiting for transfers between devices, from_behind(): return lax.ppermute(block, axis, route)  29.7 us
    ppermute x3, starting transfers between devices, from_behind(): return lax.ppermute(block, axis, route)  18.7 us
    dot_general x2, matrix products, update(): jnp.einsum('kgtn,nkd->kgtd', weights.astype(jnp.bfloat16), value_rows, pr...  10.8 us
    unnamed x11, local copies, waits for them, and re-layouts  7.88 us
    ppermute x1, starting transfers between devices, swapped(): return lax.ppermute(block, axis, route)  3.33 us
    reduce_sum x2, other arithmetic, update(): summed = summed * shrink + jnp.sum(weights, axis=-1)  3.25 us
    while x1, local copies, waits for them, and re-layouts, per_device(): running, _ = lax.fori_loop(1, reach + 1, advance, (running, paired))  3.23 us
    mul x1, other arithmetic, relative_gap(): return jnp.transpose(jnp.mean(difference * difference, axis=-1) / scale_sum)  2.47 us
  transfers between devices with their start and end apart: 4, of which 4 were waited for; matrix products, arithmetic and copies ran while one was open for 2% of the time, Pallas kernels for 0%

commit v1 on v0

--- a/solution.py
+++ b/solution.py
@@ -3,6 +3,8 @@
 import jax
 import jax.numpy as jnp
 from jax import lax
+from jax.experimental import pallas as pl
+from jax.experimental.pallas import tpu as pltpu
 from jax.sharding import PartitionSpec as P
 
 HEADS = 40
@@ -34,7 +36,7 @@
     return jnp.transpose(jnp.mean(difference * difference, axis=-1) / scale_sum)
 
 
-def per_device(queries, keys, values, lengths):
+def per_device_general(queries, keys, values, lengths):
     tokens_here = queries.shape[1]
     width_here = keys.shape[2]
     kv_local = width_here // HEAD_DIM
@@ -98,7 +100,7 @@
         return (absorb(inner, moving, (row_pos - step_id) * tokens_here), moving)
 
     running, _ = lax.fori_loop(1, reach + 1, advance, (running, paired))
-    best, summed, accum = running
+    _, summed, accum = running
     mixed = accum / summed[..., None]
     outputs = (
         jnp.transpose(mixed, (2, 0, 1, 3))
@@ -118,6 +120,272 @@
     return (outputs, gap)
 
 
+SCALE = math.log2(math.e) / math.sqrt(HEAD_DIM)
+GROUP = HEADS // KV_HEADS
+NT = (((1,), (1,)), ((), ()))
+VMEM = pl.BlockSpec(memory_space=pltpu.VMEM)
+SMEM = pl.BlockSpec(memory_space=pltpu.SMEM)
+HBM = pl.BlockSpec(memory_space=pltpu.HBM)
+
+
+def lanes(index, width):
+    if isinstance(index, int):
+        return pl.ds(index * width, width)
+    return pl.ds(pl.multiple_of(index * width, width), width)
+
+
+def twice(part):
+    return jnp.concatenate([part, part], axis=1)
+
+
+def weights_of(scores, top):
+    return jnp.exp2(scores * SCALE - top * SCALE)
+
+
+def with_ones(value_rows):
+    return jnp.concatenate([value_rows, jnp.ones_like(value_rows)], axis=1)
+
+
+def scores_of(query_rows, key_rows):
+    return lax.dot_general(query_rows, key_rows, NT, preferred_element_type=jnp.float32)
+
+
+def diagonal_kernel(
+    len_ref, q_hbm, k_hbm, v_hbm, q_ref, acc_ref, top_ref, near_ref, far_ref, k_ref, v_ref, sem
+):
+    tokens_here = q_ref.shape[0]
+    half = tokens_here // 2
+    kv_local = k_ref.shape[1] // HEAD_DIM
+    copies = [
+        pltpu.make_async_copy(k_hbm.at[0], k_ref, sem.at[0]),
+        pltpu.make_async_copy(v_hbm.at[0], v_ref, sem.at[1]),
+    ]
+    for kv in range(kv_local):
+        cols = lanes(kv, GROUP * HEAD_DIM)
+        copies.append(
+            pltpu.make_async_copy(q_hbm.at[0, :, cols], q_ref.at[:, cols], sem.at[2 + kv])
+        )
+    for copy in (copies[0], copies[2], copies[1], *copies[3:]):
+        copy.start()
+    boundary = len_ref[0] - lax.axis_index("row") * tokens_here
+    query = lax.broadcasted_iota(jnp.int32, (tokens_here, tokens_here), 0)
+    key = lax.broadcasted_iota(jnp.int32, (tokens_here, tokens_here), 1)
+    for hops, ref in ((1, near_ref), (2, far_ref)):
+        exists = lax.axis_index("row") >= hops
+        kept = (query < boundary) | (key - hops * tokens_here >= boundary)
+        ref[...] = jnp.where(kept & exists, 0.0, -jnp.inf)
+    kept = (key <= query) & ((query < boundary) | (key >= boundary))
+    bias = jnp.where(kept, 0.0, -jnp.inf)
+    copies[0].wait()
+    for kv in range(kv_local):
+        copies[2 + kv].wait()
+        if kv == 0:
+            copies[1].wait()
+        key_rows = k_ref[:, lanes(kv, HEAD_DIM)]
+        value_rows = with_ones(v_ref[:, lanes(kv, HEAD_DIM)])
+        for g in range(GROUP):
+            head = kv * GROUP + g
+            for low in (0, half):
+                rows = pl.ds(low, half)
+                seen = low + half
+                scores = scores_of(q_ref[rows, lanes(head, HEAD_DIM)], key_rows[:seen])
+                scores += bias[low:seen, :seen]
+                top = jnp.max(scores, axis=1, keepdims=True)
+                mass = weights_of(scores, top).astype(jnp.bfloat16)
+                acc_ref[rows, lanes(head, 2 * HEAD_DIM)] = jnp.dot(
+                    mass, value_rows[:seen], preferred_element_type=jnp.float32
+                )
+                top_ref[rows, lanes(head, HEAD_DIM)] = jnp.broadcast_to(top, (half, HEAD_DIM))
+
+
+def absorb(query_rows, key_rows, value_rows, bias, old_acc, old_top):
+    scores = scores_of(query_rows, key_rows) + bias
+    top = jnp.maximum(old_top, jnp.max(scores, axis=1, keepdims=True))
+    mass = weights_of(scores, twice(top)).astype(jnp.bfloat16)
+    part = jnp.dot(mass, value_rows, preferred_element_type=jnp.float32)
+    return old_acc * twice(weights_of(old_top, top)) + part, top
+
+
+def near_kernel(own, q_ref, kv_ref, acc_in, top_in, bias_ref, acc_ref, top_ref):
+    mp = lax.axis_index("mp")
+    heads_half = top_ref.shape[1] // HEAD_DIM
+    first_head = (mp if own else 1 - mp) * heads_half
+    bias = bias_ref[...]
+    for local in range(heads_half):
+        kv = local // GROUP
+        if local % GROUP == 0:
+            key_rows = kv_ref[0, :, lanes(kv, HEAD_DIM)]
+            value_rows = with_ones(kv_ref[1, :, lanes(kv, HEAD_DIM)])
+        head = first_head + local
+        acc, top = absorb(
+            q_ref[:, lanes(head, HEAD_DIM)],
+            key_rows,
+            value_rows,
+            bias,
+            acc_in[:, lanes(head, 2 * HEAD_DIM)],
+            top_in[:, lanes(head, HEAD_DIM)],
+        )
+        acc_ref[:, lanes(local, 2 * HEAD_DIM)] = acc
+        top_ref[:, lanes(local, HEAD_DIM)] = top
+
+
+def far_heads(first_head, q_ref, kv_ref, acc_ref, top_ref, bias_ref, store):
+    bias = bias_ref[...]
+    for local in range(top_ref.shape[1] // HEAD_DIM):
+        kv = local // GROUP
+        if local % GROUP == 0:
+            key_rows = kv_ref[0, :, lanes(kv, HEAD_DIM)]
+            value_rows = with_ones(kv_ref[1, :, lanes(kv, HEAD_DIM)])
+        acc, _ = absorb(
+            q_ref[:, lanes(first_head + local, HEAD_DIM)],
+            key_rows,
+            value_rows,
+            bias,
+            acc_ref[:, lanes(local, 2 * HEAD_DIM)],
+            top_ref[:, lanes(local, HEAD_DIM)],
+        )
+        store(local, (acc[:, :HEAD_DIM] / acc[:, HEAD_DIM:]).astype(jnp.bfloat16))
+
+
+def far_other_kernel(q_ref, kv_ref, acc_ref, top_ref, bias_ref, out_ref):
+    heads_half = out_ref.shape[2] // HEAD_DIM
+
+    def store(local, block):
+        out_ref[0, :, lanes(local, HEAD_DIM)] = block
+
+    first_head = (1 - lax.axis_index("mp")) * heads_half
+    far_heads(first_head, q_ref, kv_ref, acc_ref, top_ref, bias_ref, store)
+
+
+def far_own_kernel(
+    q_ref, kv_ref, acc_ref, top_ref, bias_ref, sent_ref, got_ref, out_ref, gap_ref, mine_ref, sem
+):
+    width = sent_ref.shape[2]
+    heads_half = width // HEAD_DIM
+    mp = lax.axis_index("mp")
+    copies = [
+        pltpu.make_async_copy(sent_ref.at[0], out_ref.at[0, :, lanes(1 - mp, width)], sem.at[0])
+    ]
+    copies[0].start()
+    mean = jnp.full((16, HEAD_DIM), 1.0 / HEAD_DIM, jnp.bfloat16)
+
+    def store(local, block):
+        mine_ref[:, lanes(local, HEAD_DIM)] = block
+        if local % GROUP == GROUP - 1:
+            step = local // GROUP
+            cols = lanes(step, GROUP * HEAD_DIM)
+            spot = lanes(mp * (heads_half // GROUP) + step, GROUP * HEAD_DIM)
+            copy = pltpu.make_async_copy(
+                mine_ref.at[:, cols], out_ref.at[0, :, spot], sem.at[1 + step]
+            )
+            copy.start()
+            copies.append(copy)
+        mine = block.astype(jnp.float32)
+        theirs = got_ref[0, :, lanes(local, HEAD_DIM)].astype(jnp.float32)
+        difference = mine - theirs
+        policy = jnp.where(mp == 0, mine, theirs)
+        squares = jnp.concatenate([difference * difference, policy * policy], axis=0)
+        means = scores_of(mean, squares.astype(jnp.bfloat16))
+        tokens_here = block.shape[0]
+        gap_ref[local : local + 1, :] = means[:1, :tokens_here] / (
+            means[:1, tokens_here:] + 1e-06
+        )
+
+    far_heads(mp * heads_half, q_ref, kv_ref, acc_ref, top_ref, bias_ref, store)
+    for copy in copies:
+        copy.wait()
+
+
+def call(kernel, out_shape, in_specs, out_specs, flops, **more):
+    return pl.pallas_call(
+        kernel,
+        out_shape=out_shape,
+        in_specs=in_specs,
+        out_specs=out_specs,
+        cost_estimate=pl.CostEstimate(
+            flops=int(flops), bytes_accessed=4 << 20, transcendentals=0
+        ),
+        compiler_params=pltpu.CompilerParams(vmem_limit_bytes=16 * 2**20),
+        **more,
+    )
+
+
+def per_device_paired(queries, keys, values, lengths):
+    tokens_here = queries.shape[1]
+    kv_local = keys.shape[2] // HEAD_DIM
+    heads_local = kv_local * GROUP
+    width = heads_local * HEAD_DIM
+    half = width // 2
+    half_kv = keys.shape[2] // 2
+    count = lax.axis_size("row")
+    mp = lax.axis_index("mp")
+    f32, bf16 = jnp.float32, jnp.bfloat16
+    shape = jax.ShapeDtypeStruct
+    bias_type = shape((tokens_here, tokens_here), f32)
+    work = 8 * heads_local * tokens_here * tokens_here * HEAD_DIM
+
+    def pack(which):
+        parts = [lax.dynamic_slice_in_dim(x, which * half_kv, half_kv, 2) for x in (keys, values)]
+        return jnp.concatenate(parts, axis=0)
+
+    near_route = [(i - 1, i) for i in range(1, count)]
+    far_route = [(i - 1, i) for i in range(2, count)]
+    other_near = lax.ppermute(pack(1 - mp), "row", near_route)
+    own_near = lax.ppermute(pack(mp), "row", near_route)
+    query_rows, acc, top, near_bias, far_bias = call(
+        diagonal_kernel,
+        (
+            shape((tokens_here, width), bf16),
+            shape((tokens_here, 2 * width), f32),
+            shape((tokens_here, width), f32),
+            bias_type,
+            bias_type,
+        ),
+        [SMEM] + [HBM] * 3,
+        [VMEM] * 5,
+        work,
+        scratch_shapes=[
+            pltpu.VMEM((tokens_here, keys.shape[2]), bf16),
+            pltpu.VMEM((tokens_here, keys.shape[2]), bf16),
+            pltpu.SemaphoreType.DMA((2 + kv_local,)),
+        ],
+    )(lengths, queries, keys, values)
+    other_far = lax.ppermute(other_near, "row", far_route)
+    state_type = (shape((tokens_here, width), f32), shape((tokens_here, half), f32))
+
+    def near(own, block):
+        return call(
+            lambda *refs: near_kernel(own, *refs), state_type, [VMEM] * 5, [VMEM] * 2, work
+        )(query_rows, block, acc, top, near_bias)
+
+    other_state = near(False, other_near)
+    own_far = lax.ppermute(own_near, "row", far_route)
+    own_state = near(True, own_near)
+    sent = call(
+        far_other_kernel, shape((1, tokens_here, half), bf16), [VMEM] * 5, VMEM, work
+    )(query_rows, other_far, *other_state, far_bias)
+    got = lax.ppermute(sent, "mp", [(0, 1), (1, 0)])
+    outputs, gap = call(
+        far_own_kernel,
+        (
+            shape((1, tokens_here, width), bf16),
+            shape((heads_local // 2, tokens_here), f32),
+        ),
+        [VMEM] * 7,
+        [HBM, VMEM],
+        work,
+        scratch_shapes=[
+            pltpu.VMEM((tokens_here, half), bf16),
+            pltpu.SemaphoreType.DMA((1 + kv_local // 2,)),
+        ],
+    )(query_rows, own_far, *own_state, far_bias, sent, got)
+    return (outputs, gap)
+
+
+def two_hops(mesh, rollouts):
+    return rollouts == 2 and mesh.shape["row"] // 2 == 2 and mesh.shape["mp"] == 2
+
+
 def solution(mesh):
     in_specs = (
         P("mp", ("groups", "row"), "col"),
@@ -126,6 +394,17 @@
         P("groups"),
     )
     out_specs = (P("mp", ("groups", "row"), "col"), P(("col", "mp"), ("groups", "row")))
-    return jax.shard_map(
-        per_device, mesh=mesh, in_specs=in_specs, out_specs=out_specs, check_vma=False
-    )
+
+    def place(body):
+        return jax.shard_map(
+            body, mesh=mesh, in_specs=in_specs, out_specs=out_specs, check_vma=False
+        )
+
+    def step(queries, keys, values, lengths):
+        rollouts = lengths.shape[0] // mesh.shape["groups"]
+        kv_local = keys.shape[2] // HEAD_DIM // mesh.shape["col"]
+        if not two_hops(mesh, rollouts) or kv_local % 2:
+            return place(per_device_general)(queries, keys, values, lengths)
+        return place(per_device_paired)(queries, keys, values, lengths)
+
+    return step

time: 104 us -> 49.9 us (0.48)
  the two profiles are of different devices: /device:TPU:17 before, /device:TPU:20 now
where the time goes in v1:
time: 49.9 us; the launch traced here: 49.7 us
  waiting for transfers between devices  20.7 us (41%)
  Pallas kernels  14 us (28%)
  starting transfers between devices  11.6 us (23%)
  local copies, waits for them, and re-layouts  2.51 us (5%)
  between operations  0.79 us (2%)
    ppermute x1, waiting for transfers between devices, per_device_paired(): own_near = lax.ppermute(pack(mp), 'row', near_route)  8.27 us
    ppermute x1, waiting for transfers between devices, per_device_paired(): other_near = lax.ppermute(pack(1 - mp), 'row', near_route)  6.45 us
    ppermute x1, waiting for transfers between devices, per_device_paired(): own_far = lax.ppermute(own_near, 'row', far_route)  5.98 us
    pallas_call x1, Pallas kernels, per_device_paired(): call(far_own_kernel, (shape((1, tokens_here, width), bf16), shape((heads_...  5.79 us
    pallas_call x1, Pallas kernels, per_device_paired(): call(diagonal_kernel, (shape((tokens_here, width), bf16), shape((tokens_h...  3.95 us
    ppermute x1, starting transfers between devices, per_device_paired(): other_near = lax.ppermute(pack(1 - mp), 'row', near_route)  3.48 us
    ppermute x1, starting transfers between devices, per_device_paired(): other_far = lax.ppermute(other_near, 'row', far_route)  3.47 us
    pallas_call x2, Pallas kernels, near(): call(lambda *refs: near_kernel(own, *refs), state_type, [VMEM] * 5, [VMEM...  2.87 us
  transfers between devices with their start and end apart: 5, of which 3 were waited for; matrix products, arithmetic and copies ran while one was open for 0% of the time, Pallas kernels for 14%

profile of v1, /device:TPU:20, one launch (start us, length us, event | category | flops | bytes accessed | tf_op | source)
XLA Modules:
  0.0 49.7 jit_solution(4289578657553318984)
XLA Ops:
  0.6 0.0 copy-start
  0.6 0.0 copy-start.1
  0.7 0.0 copy-start.3
  0.7 1.2 %constant_dynamic-slice_fusion = (bf16[1,256,256]{2,1,0:T(8,128)(2,1)S(1)}, bf16[1,256,256]{2,1,0:T(8,128)(2,1)S(1)}, bf16[1,256,256]{2,1,0:T(8,128)(2,1)S(1)}, bf16[1,256,256]{2,1,0:T(8,128)(2,1)S(1)}) fusion(bf16[1,256,512]{2,1,0:T(8,128)(2,1)} %v_hbm.1, s32[]{:T(128)S(6)} %select_n.9, s32[]{:T(128)S(6)} %select_n.8, bf16[1,256,512]{2,1,0:T(8,128)(2,1)} %k_hbm.1), kind=kLoop, calls=%fused_computation.2 | loop fusion | bytes 1048584 | tf_op jit(solution)/shard_map/dynamic_slice | solution.py:328
  1.9 3.5 %collective-permute-start.2 = (bf16[2,256,256]{2,1,0:T(8,128)(2,1)S(1)}, bf16[2,256,256]{2,1,0:T(8,128)(2,1)S(1)}, u32[]{:S(2)}, u32[]{:S(2)}) collective-permute-start(bf16[2,256,256]{2,1,0:T(8,128)(2,1)S(1)} %pad_maximum_fusion.1), channel_id=1, source_target_pairs={{0,4},{4,8},{8,12},{1,5},{5,9},{9,13},{2,6},{6,10},{10,14},{3,7},{... | collective-permute-start | bytes 786440 | tf_op jit(solution)/shard_map/ppermute | solution.py:333
  5.4 6.4 %collective-permute-done.2.refs_1_ = bf16[2,256,256]{2,1,0:T(8,128)(2,1)S(1)} collective-permute-done((bf16[2,256,256]{2,1,0:T(8,128)(2,1)S(1)}, bf16[2,256,256]{2,1,0:T(8,128)(2,1)S(1)}, u32[]{:S(2)}, u32[]{:S(2)}) %collective-permute-start.2) | collective-permute-done | bytes 262176 | tf_op jit(solution)/shard_map/ppermute | solution.py:333
  11.8 3.5 %collective-permute-start.3 = (bf16[2,256,256]{2,1,0:T(8,128)(2,1)S(1)}, bf16[2,256,256]{2,1,0:T(8,128)(2,1)S(1)}, u32[]{:S(2)}, u32[]{:S(2)}) collective-permute-start(bf16[2,256,256]{2,1,0:T(8,128)(2,1)S(1)} %collective-permute-done.2.refs_1_), channel_id=1, source_target_pairs={{4,8},{8,12},{5,9},{9,13},{6,10},{10,14},{7,11},{11,15},{20,24},{2... | collective-permute-start | bytes 786440 | tf_op jit(solution)/shard_map/ppermute | solution.py:353
  15.3 0.0 copy-done
  15.3 0.0 copy-done.1
  15.3 0.0 copy-done.3
  15.3 0.0 copy-start.2
  15.4 1.3 %copy-done.2 = bf16[1,256,2560]{2,1,0:T(8,128)(2,1)S(1)} copy-done((bf16[1,256,2560]{2,1,0:T(8,128)(2,1)S(1)}, bf16[1,256,2560]{2,1,0:T(8,128)(2,1)}, u32[]{:S(2)}) %copy-start.2) | copy-done | bytes 1310744
  16.7 3.9 %shard_map.59 = (bf16[256,2560]{1,0:T(8,128)(2,1)S(1)}, f32[256,5120]{1,0:T(8,128)S(1)}, f32[256,2560]{1,0:T(8,128)S(1)}, f32[256,256]{1,0:T(8,128)S(1)}, f32[256,256]{1,0:T(8,128)S(1)}) custom-call(s32[2]{0:T(128)S(1)} %copy-done.3, bf16[1,256,2560]{2,1,0:T(8,128)(2,1)S(1)} %copy-done.2, bf16[1,256,512]{2,1,0:T(8,128)(2,1)S(1)} %copy-done, ...), custom_call_target="tpu_custom_call" | custom-call | flops 1342177280 | bytes 4194304 | tf_op jit(solution)/shard_map/pallas_call | solution.py:335
  20.6 1.4 %shard_map.61 = (f32[256,2560]{1,0:T(8,128)S(1)}, f32[256,1280]{1,0:T(8,128)S(1)}) custom-call(bf16[256,2560]{1,0:T(8,128)(2,1)S(1)} %get-tuple-element.11.refs_0_.q_ref, bf16[2,256,256]{2,1,0:T(8,128)(2,1)S(1)} %collective-permute-done.2.refs_1_, f32[256,5120]{1,0:T(8,128)S(1)} %get-tuple-element.12.refs_2_, f32[256,2560]{1,0:T(8,128)S(1)} %get-tuple-element.13.refs_3_, ...), custom_call_target="tpu_custom_call" | custom-call | flops 1342177280 | bytes 4194304 | tf_op jit(solution)/shard_map/pallas_call | solution.py:357
  22.1 0.0 collective-permute-done.3.kv_ref
  22.1 1.4 %shard_map.62.sent_ref = bf16[1,256,1280]{2,1,0:T(8,128)(2,1)S(1)} custom-call(bf16[256,2560]{1,0:T(8,128)(2,1)S(1)} %get-tuple-element.11.refs_0_.q_ref, bf16[2,256,256]{2,1,0:T(8,128)(2,1)S(1)} %collective-permute-done.3.kv_ref, f32[256,2560]{1,0:T(8,128)S(1)} %get-tuple-element.18.acc_ref, f32[256,1280]{1,0:T(8,128)S(1)} %get-tuple-element.19.top_ref, ...), custom_call_target="tpu_custom_call" | custom-call | flops 1342177280 | bytes 4194304 | tf_op jit(solution)/shard_map/pallas_call | solution.py:364
  23.5 0.1 collective-permute-start.4
  23.6 2.3 %collective-permute-start = (bf16[2,256,256]{2,1,0:T(8,128)(2,1)S(1)}, bf16[2,256,256]{2,1,0:T(8,128)(2,1)S(1)}, u32[]{:S(2)}, u32[]{:S(2)}) collective-permute-start(bf16[2,256,256]{2,1,0:T(8,128)(2,1)S(1)} %pad_maximum_fusion), channel_id=1, source_target_pairs={{0,4},{4,8},{8,12},{1,5},{5,9},{9,13},{2,6},{6,10},{10,14},{3,7},{... | collective-permute-start | bytes 786440 | tf_op jit(solution)/shard_map/ppermute | solution.py:334
  25.9 8.3 %collective-permute-done.refs_1_ = bf16[2,256,256]{2,1,0:T(8,128)(2,1)S(1)} collective-permute-done((bf16[2,256,256]{2,1,0:T(8,128)(2,1)S(1)}, bf16[2,256,256]{2,1,0:T(8,128)(2,1)S(1)}, u32[]{:S(2)}, u32[]{:S(2)}) %collective-permute-start) | collective-permute-done | bytes 262176 | tf_op jit(solution)/shard_map/ppermute | solution.py:334
  34.2 2.3 %collective-permute-start.1 = (bf16[2,256,256]{2,1,0:T(8,128)(2,1)S(1)}, bf16[2,256,256]{2,1,0:T(8,128)(2,1)S(1)}, u32[]{:S(2)}, u32[]{:S(2)}) collective-permute-start(bf16[2,256,256]{2,1,0:T(8,128)(2,1)S(1)} %collective-permute-done.refs_1_), channel_id=1, source_target_pairs={{4,8},{8,12},{5,9},{9,13},{6,10},{10,14},{7,11},{11,15},{20,24},{2... | collective-permute-start | bytes 786440 | tf_op jit(solution)/shard_map/ppermute | solution.py:362
  36.5 1.4 %shard_map.60 = (f32[256,2560]{1,0:T(8,128)S(1)}, f32[256,1280]{1,0:T(8,128)S(1)}) custom-call(bf16[256,2560]{1,0:T(8,128)(2,1)S(1)} %get-tuple-element.11.refs_0_.q_ref, bf16[2,256,256]{2,1,0:T(8,128)(2,1)S(1)} %collective-permute-done.refs_1_, f32[256,5120]{1,0:T(8,128)S(1)} %get-tuple-element.12.refs_2_, f32[256,2560]{1,0:T(8,128)S(1)} %get-tuple-element.13.refs_3_, ...), custom_call_target="tpu_custom_call" | custom-call | flops 1342177280 | bytes 4194304 | tf_op jit(solution)/shard_map/pallas_call | solution.py:357
  37.9 6.0 %collective-permute-done.1.kv_ref = bf16[2,256,256]{2,1,0:T(8,128)(2,1)S(1)} collective-permute-done((bf16[2,256,256]{2,1,0:T(8,128)(2,1)S(1)}, bf16[2,256,256]{2,1,0:T(8,128)(2,1)S(1)}, u32[]{:S(2)}, u32[]{:S(2)}) %collective-permute-start.1) | collective-permute-done | bytes 262176 | tf_op jit(solution)/shard_map/ppermute | solution.py:362
  43.9 0.0 collective-permute-done.4.got_ref
  43.9 5.8 %shard_map.63 = (bf16[1,256,2560]{2,1,0:T(8,128)(2,1)}, f32[10,256]{1,0:T(8,128)}) custom-call(bf16[256,2560]{1,0:T(8,128)(2,1)S(1)} %get-tuple-element.11.refs_0_.q_ref, bf16[2,256,256]{2,1,0:T(8,128)(2,1)S(1)} %collective-permute-done.1.kv_ref, f32[256,2560]{1,0:T(8,128)S(1)} %get-tuple-element.15.acc_ref, f32[256,1280]{1,0:T(8,128)S(1)} %get-tuple-element.16.top_ref, ...), custom_call_target="tpu_custom_call" | custom-call | flops 1342177280 | bytes 4194304 | tf_op jit(solution)/shard_map/pallas_call | solution.py:368
  (2 shorter events, 0.1 us)
Async XLA Ops:
  0.6 14.7 %copy-start = (bf16[1,256,512]{2,1,0:T(8,128)(2,1)S(1)}, bf16[1,256,512]{2,1,0:T(8,128)(2,1)}, u32[]{:S(2)}) copy-start(bf16[1,256,512]{2,1,0:T(8,128)(2,1)} %k_hbm.1) | copy-start | bytes 786436
  0.6 14.7 %copy-start.1 = (bf16[1,256,512]{2,1,0:T(8,128)(2,1)S(1)}, bf16[1,256,512]{2,1,0:T(8,128)(2,1)}, u32[]{:S(2)}) copy-start(bf16[1,256,512]{2,1,0:T(8,128)(2,1)} %v_hbm.1) | copy-start | bytes 786436
  0.7 14.7 %copy-start.3 = (s32[2]{0:T(128)S(1)}, s32[2]{0:T(128)}, u32[]{:S(2)}) copy-start(s32[2]{0:T(128)} %len_ref.1) | copy-start | bytes 28
  1.9 9.9 %collective-permute-start.2 = (bf16[2,256,256]{2,1,0:T(8,128)(2,1)S(1)}, bf16[2,256,256]{2,1,0:T(8,128)(2,1)S(1)}, u32[]{:S(2)}, u32[]{:S(2)}) collective-permute-start(bf16[2,256,256]{2,1,0:T(8,128)(2,1)S(1)} %pad_maximum_fusion.1), channel_id=1, source_target_pairs={{0,4},{4,8},{8,12},{1,5},{5,9},{9,13},{2,6},{6,10},{10,14},{3,7},{... | collective-permute-start | bytes 786440 | tf_op jit(solution)/shard_map/ppermute | solution.py:333
  11.8 10.2 %collective-permute-start.3 = (bf16[2,256,256]{2,1,0:T(8,128)(2,1)S(1)}, bf16[2,256,256]{2,1,0:T(8,128)(2,1)S(1)}, u32[]{:S(2)}, u32[]{:S(2)}) collective-permute-start(bf16[2,256,256]{2,1,0:T(8,128)(2,1)S(1)} %collective-permute-done.2.refs_1_), channel_id=1, source_target_pairs={{4,8},{8,12},{5,9},{9,13},{6,10},{10,14},{7,11},{11,15},{20,24},{2... | collective-permute-start | bytes 786440 | tf_op jit(solution)/shard_map/ppermute | solution.py:353
  15.3 1.3 %copy-start.2 = (bf16[1,256,2560]{2,1,0:T(8,128)(2,1)S(1)}, bf16[1,256,2560]{2,1,0:T(8,128)(2,1)}, u32[]{:S(2)}) copy-start(bf16[1,256,2560]{2,1,0:T(8,128)(2,1)} %q_hbm.1) | copy-start | bytes 3932164
  23.5 20.4 %collective-permute-start.4 = (bf16[1,256,1280]{2,1,0:T(8,128)(2,1)S(1)}, bf16[1,256,1280]{2,1,0:T(8,128)(2,1)S(1)}, u32[]{:S(2)}, u32[]{:S(2)}) collective-permute-start(bf16[1,256,1280]{2,1,0:T(8,128)(2,1)S(1)} %shard_map.62.sent_ref), channel_id=1, source_target_pairs={{0,1},{1,0},{2,3},{3,2},{4,5},{5,4},{6,7},{7,6},{8,9},{9,8},{10,11... | collective-permute-start | bytes 1966088 | tf_op jit(solution)/shard_map/ppermute | solution.py:367
  23.6 10.6 %collective-permute-start = (bf16[2,256,256]{2,1,0:T(8,128)(2,1)S(1)}, bf16[2,256,256]{2,1,0:T(8,128)(2,1)S(1)}, u32[]{:S(2)}, u32[]{:S(2)}) collective-permute-start(bf16[2,256,256]{2,1,0:T(8,128)(2,1)S(1)} %pad_maximum_fusion), channel_id=1, source_target_pairs={{0,4},{4,8},{8,12},{1,5},{5,9},{9,13},{2,6},{6,10},{10,14},{3,7},{... | collective-permute-start | bytes 786440 | tf_op jit(solution)/shard_map/ppermute | solution.py:334
  34.2 9.7 %collective-permute-start.1 = (bf16[2,256,256]{2,1,0:T(8,128)(2,1)S(1)}, bf16[2,256,256]{2,1,0:T(8,128)(2,1)S(1)}, u32[]{:S(2)}, u32[]{:S(2)}) collective-permute-start(bf16[2,256,256]{2,1,0:T(8,128)(2,1)S(1)} %collective-permute-done.refs_1_), channel_id=1, source_target_pairs={{4,8},{8,12},{5,9},{9,13},{6,10},{10,14},{7,11},{11,15},{20,24},{2... | collective-permute-start | bytes 786440 | tf_op jit(solution)/shard_map/ppermute | solution.py:362

commit v2 on v0

--- a/solution.py
+++ b/solution.py
@@ -3,6 +3,8 @@
 import jax
 import jax.numpy as jnp
 from jax import lax
+from jax.experimental import pallas as pl
+from jax.experimental.pallas import tpu as pltpu
 from jax.sharding import PartitionSpec as P
 
 HEADS = 40
@@ -34,7 +36,7 @@
     return jnp.transpose(jnp.mean(difference * difference, axis=-1) / scale_sum)
 
 
-def per_device(queries, keys, values, lengths):
+def per_device_general(queries, keys, values, lengths):
     tokens_here = queries.shape[1]
     width_here = keys.shape[2]
     kv_local = width_here // HEAD_DIM
@@ -98,7 +100,7 @@
         return (absorb(inner, moving, (row_pos - step_id) * tokens_here), moving)
 
     running, _ = lax.fori_loop(1, reach + 1, advance, (running, paired))
-    best, summed, accum = running
+    _, summed, accum = running
     mixed = accum / summed[..., None]
     outputs = (
         jnp.transpose(mixed, (2, 0, 1, 3))
@@ -118,6 +120,345 @@
     return (outputs, gap)
 
 
+SCALE = math.log2(math.e) / math.sqrt(HEAD_DIM)
+GROUP = HEADS // KV_HEADS
+BIG = 2.0**100
+LIMIT = 2.0**100
+NT = (((1,), (1,)), ((), ()))
+VMEM = pl.BlockSpec(memory_space=pltpu.VMEM)
+SMEM = pl.BlockSpec(memory_space=pltpu.SMEM)
+HBM = pl.BlockSpec(memory_space=pltpu.HBM)
+
+
+def lanes(index, width):
+    if isinstance(index, int):
+        return pl.ds(index * width, width)
+    return pl.ds(pl.multiple_of(index * width, width), width)
+
+
+def with_ones(value_rows):
+    return jnp.concatenate([value_rows, jnp.ones_like(value_rows)], axis=1)
+
+
+def scores_of(query_rows, key_rows):
+    return lax.dot_general(query_rows, key_rows, NT, preferred_element_type=jnp.float32)
+
+
+def mass_of(scores):
+    return jnp.exp2(scores * SCALE).astype(jnp.bfloat16)
+
+
+def spread(mass, value_rows):
+    return jnp.dot(mass, value_rows, preferred_element_type=jnp.float32)
+
+
+def in_columns(shape, *columns):
+    lane = lax.broadcasted_iota(jnp.int32, shape, 1)
+    tile = jnp.zeros(shape, jnp.float32)
+    for index, column in enumerate(columns):
+        tile = jnp.where(lane == index, column, tile)
+    return tile
+
+
+def diagonal_kernel(
+    len_hbm, q_hbm, other_ref, own_ref, wide_ref, acc_ref, near_ref, far_ref, bias_ref, q_ref,
+    len_ref, sem
+):
+    tokens_here = q_ref.shape[0]
+    half = tokens_here // 2
+    mp = lax.axis_index("mp")
+    row_pos = lax.axis_index("row")
+    kv_half = other_ref.shape[2] // HEAD_DIM
+    spot = GROUP * HEAD_DIM
+    len_copy = pltpu.make_async_copy(len_hbm, len_ref, sem.at[2 * kv_half])
+    len_copy.start()
+    copies = []
+    for step in range(2 * kv_half):
+        which = 1 - mp if step < kv_half else mp
+        copies.append(
+            pltpu.make_async_copy(
+                q_hbm.at[0, :, lanes(which * kv_half + step % kv_half, spot)],
+                q_ref.at[:, lanes(step, spot)],
+                sem.at[step],
+            )
+        )
+        copies[step].start()
+    len_copy.wait()
+    boundary = len_ref[0] - row_pos * tokens_here
+    query = lax.broadcasted_iota(jnp.int32, (tokens_here, tokens_here), 0)
+    key = lax.broadcasted_iota(jnp.int32, (tokens_here, tokens_here), 1)
+    kept = (key <= query) & ((query < boundary) | (key >= boundary))
+    bias_ref[...] = jnp.where(kept, 0.0, -jnp.inf)
+    tile = (tokens_here, HEAD_DIM)
+    token = lax.broadcasted_iota(jnp.int32, tile, 0)
+    for hops, ref in ((1, near_ref), (2, far_ref)):
+        gone = jnp.where(row_pos >= hops, 0.0, -BIG)
+        before = jnp.where(token - hops * tokens_here < boundary, -BIG, 0.0)
+        ref[...] = in_columns(tile, -1.0, before, gone).astype(jnp.bfloat16)
+    later = in_columns(tile, 0.0, jnp.where(token >= boundary, 1.0, 0.0), 1.0)
+    first_lane = lax.broadcasted_iota(jnp.int32, (half, HEAD_DIM), 1) == 0
+    for step in range(2 * kv_half):
+        copies[step].wait()
+        pack_ref = other_ref if step < kv_half else own_ref
+        key_rows = pack_ref[0, :, lanes(step % kv_half, HEAD_DIM)]
+        value_rows = value_of(pack_ref, step % kv_half)
+        for g in range(GROUP):
+            local = step * GROUP + g
+            for low in (0, half):
+                rows = pl.ds(low, half)
+                seen = low + half
+                query_rows = q_ref[rows, lanes(local, HEAD_DIM)]
+                scores = scores_of(query_rows, key_rows[:seen]) + bias_ref[rows, :seen]
+                top = jnp.max(scores, axis=1, keepdims=True).astype(jnp.bfloat16)
+                top = top.astype(jnp.float32)
+                acc_ref[rows, lanes(local, 2 * HEAD_DIM)] = spread(
+                    mass_of(scores - top), value_rows[:seen]
+                )
+                extra = jnp.where(first_lane, top, later[low:seen]).astype(jnp.bfloat16)
+                wide_ref[rows, lanes(2 * local, HEAD_DIM)] = query_rows
+                wide_ref[rows, lanes(2 * local + 1, HEAD_DIM)] = extra
+
+
+def key_of(kv_ref, kv, tile_ref):
+    return jnp.concatenate([kv_ref[0, :, lanes(kv, HEAD_DIM)], tile_ref[...]], axis=1)
+
+
+def value_of(kv_ref, kv):
+    return with_ones(kv_ref[1, :, lanes(kv, HEAD_DIM)])
+
+
+def near_kernel(own, wide_ref, kv_ref, acc_in, tile_ref, acc_ref):
+    heads_half = acc_ref.shape[1] // (2 * HEAD_DIM)
+    first_head = heads_half if own else 0
+    for local in range(heads_half):
+        if local % GROUP == 0:
+            key_rows = key_of(kv_ref, local // GROUP, tile_ref)
+            value_rows = value_of(kv_ref, local // GROUP)
+        cols = lanes(first_head + local, 2 * HEAD_DIM)
+        mass = mass_of(scores_of(wide_ref[:, cols], key_rows))
+        acc_ref[:, lanes(local, 2 * HEAD_DIM)] = acc_in[:, cols] + spread(mass, value_rows)
+
+
+def far_heads(first_head, refs, store):
+    wide_ref, _, far_kv, _, acc_ref, _, far_tile = refs
+    worst = None
+    for local in range(acc_ref.shape[1] // (2 * HEAD_DIM)):
+        if local % GROUP == 0:
+            key_rows = key_of(far_kv, local // GROUP, far_tile)
+            value_rows = value_of(far_kv, local // GROUP)
+        mass = mass_of(scores_of(wide_ref[:, lanes(first_head + local, 2 * HEAD_DIM)], key_rows))
+        acc = acc_ref[:, lanes(local, 2 * HEAD_DIM)] + spread(mass, value_rows)
+        total = acc[:, HEAD_DIM:]
+        store(local, (acc[:, :HEAD_DIM] / total).astype(jnp.bfloat16))
+        worst = total if worst is None else jnp.maximum(worst, total)
+    return jnp.logical_not(jnp.max(worst) < LIMIT)
+
+
+def far_heads_again(first_head, refs, store):
+    wide_ref, near_kv, far_kv, first_ref, acc_ref, near_tile, far_tile = refs
+
+    @pl.loop(0, acc_ref.shape[1] // (2 * HEAD_DIM))
+    def _(local):
+        cols = lanes(first_head + local, 2 * HEAD_DIM)
+        query_rows = wide_ref[:, cols]
+        kv = local // GROUP
+        near_scores = scores_of(query_rows, key_of(near_kv, kv, near_tile))
+        far_scores = scores_of(query_rows, key_of(far_kv, kv, far_tile))
+        top = jnp.max(jnp.maximum(near_scores, far_scores), axis=1, keepdims=True)
+        top = jnp.maximum(top, 0.0)
+        acc = (
+            first_ref[:, cols] * jnp.exp2(-top * SCALE)
+            + spread(mass_of(near_scores - top), value_of(near_kv, kv))
+            + spread(mass_of(far_scores - top), value_of(far_kv, kv))
+        )
+        store(local, (acc[:, :HEAD_DIM] / acc[:, HEAD_DIM:]).astype(jnp.bfloat16))
+
+
+def far_other_kernel(*refs):
+    refs, out_ref = refs[:7], refs[7]
+    first_head = 0
+
+    def store(local, block):
+        out_ref[0, :, lanes(local, HEAD_DIM)] = block
+
+    too_high = far_heads(first_head, refs, store)
+
+    @pl.when(too_high)
+    def _():
+        far_heads_again(first_head, refs, store)
+
+
+def far_own_kernel(*refs):
+    refs, (sent_ref, got_ref, out_ref, gap_ref, mine_ref, sem) = refs[:7], refs[7:]
+    width = sent_ref.shape[2]
+    tokens_here = sent_ref.shape[1]
+    heads_half = width // HEAD_DIM
+    mp = lax.axis_index("mp")
+    first_head = heads_half
+    spot = GROUP * HEAD_DIM
+    steps = heads_half // GROUP
+    sent_copy = pltpu.make_async_copy(
+        sent_ref.at[0], out_ref.at[0, :, lanes(1 - mp, width)], sem.at[steps]
+    )
+    sent_copy.start()
+    mine_copies = [
+        pltpu.make_async_copy(
+            mine_ref.at[:, lanes(step, spot)],
+            out_ref.at[0, :, lanes(mp * steps + step, spot)],
+            sem.at[step],
+        )
+        for step in range(steps)
+    ]
+    lane = lax.broadcasted_iota(jnp.int32, (tokens_here, HEAD_DIM), 1)
+    state = {"far": jnp.zeros((tokens_here, HEAD_DIM), jnp.float32)}
+    state["size"] = state["far"]
+
+    def squares(local, block):
+        mine = block.astype(jnp.float32)
+        theirs = got_ref[0, :, lanes(local, HEAD_DIM)].astype(jnp.float32)
+        difference = mine - theirs
+        policy = jnp.where(mp == 0, mine, theirs)
+        return (
+            jnp.sum(difference * difference, axis=1, keepdims=True),
+            jnp.sum(policy * policy, axis=1, keepdims=True),
+        )
+
+    def gap_of(far, size):
+        return far.T[:heads_half] / HEAD_DIM / (size.T[:heads_half] / HEAD_DIM + 1e-06)
+
+    def store(local, block):
+        mine_ref[:, lanes(local, HEAD_DIM)] = block
+        if local % GROUP == GROUP - 1:
+            mine_copies[local // GROUP].start()
+        far, size = squares(local, block)
+        state["far"] = jnp.where(lane == local, far, state["far"])
+        state["size"] = jnp.where(lane == local, size, state["size"])
+
+    too_high = far_heads(first_head, refs, store)
+    gap_ref[...] = gap_of(state["far"], state["size"])
+    sent_copy.wait()
+    for copy in mine_copies:
+        copy.wait()
+
+    @pl.when(too_high)
+    def _():
+        def store_again(local, block):
+            mine_ref[:, lanes(local, HEAD_DIM)] = block
+
+        far_heads_again(first_head, refs, store_again)
+        far = size = jnp.zeros((tokens_here, HEAD_DIM), jnp.float32)
+        for local in range(heads_half):
+            parts = squares(local, mine_ref[:, lanes(local, HEAD_DIM)])
+            far = jnp.where(lane == local, parts[0], far)
+            size = jnp.where(lane == local, parts[1], size)
+        gap_ref[...] = gap_of(far, size)
+        for copy in mine_copies:
+            copy.start()
+        for copy in mine_copies:
+            copy.wait()
+
+
+def in_hbm(array):
+    return pltpu.with_memory_space_constraint(array, pltpu.HBM)
+
+
+def call(kernel, out_shape, in_specs, out_specs, flops, vmem_mib=16, **more):
+    return pl.pallas_call(
+        kernel,
+        out_shape=out_shape,
+        in_specs=in_specs,
+        out_specs=out_specs,
+        cost_estimate=pl.CostEstimate(
+            flops=int(flops), bytes_accessed=4 << 20, transcendentals=0
+        ),
+        compiler_params=pltpu.CompilerParams(vmem_limit_bytes=vmem_mib * 2**20),
+        **more,
+    )
+
+
+def per_device_paired(queries, keys, values, lengths):
+    tokens_here = queries.shape[1]
+    kv_local = keys.shape[2] // HEAD_DIM
+    heads_local = kv_local * GROUP
+    width = heads_local * HEAD_DIM
+    half = width // 2
+    half_kv = keys.shape[2] // 2
+    count = lax.axis_size("row")
+    mp = lax.axis_index("mp")
+    f32, bf16 = jnp.float32, jnp.bfloat16
+    shape = jax.ShapeDtypeStruct
+    tile_type = shape((tokens_here, HEAD_DIM), bf16)
+    work = 8 * heads_local * tokens_here * tokens_here * HEAD_DIM
+
+    def pack(which):
+        parts = [lax.dynamic_slice_in_dim(x, which * half_kv, half_kv, 2) for x in (keys, values)]
+        return jnp.concatenate(parts, axis=0)
+
+    near_route = [(i - 1, i) for i in range(1, count)]
+    far_route = [(i - 1, i) for i in range(2, count)]
+    other = pack(1 - mp)
+    other_near = lax.ppermute(other, "row", near_route)
+    other, which = lax.optimization_barrier((other, mp))
+    own = pack(which)
+    own_near = lax.ppermute(own, "row", near_route)
+    wide, acc, near_tile, far_tile = call(
+        diagonal_kernel,
+        (
+            shape((tokens_here, 2 * width), bf16),
+            shape((tokens_here, 2 * width), f32),
+            tile_type,
+            tile_type,
+        ),
+        [HBM] * 2 + [VMEM] * 2,
+        [VMEM] * 4,
+        work,
+        vmem_mib=16,
+        scratch_shapes=[
+            pltpu.VMEM((tokens_here, tokens_here), f32),
+            pltpu.VMEM((tokens_here, width), bf16),
+            pltpu.SMEM(lengths.shape, jnp.int32),
+            pltpu.SemaphoreType.DMA((1 + kv_local,)),
+        ],
+    )(in_hbm(lengths), in_hbm(queries), other, own)
+    other_far = lax.ppermute(other_near, "row", far_route)
+
+    def near(own, block):
+        return call(
+            lambda *refs: near_kernel(own, *refs),
+            shape((tokens_here, width), f32),
+            [VMEM] * 4,
+            VMEM,
+            work,
+        )(wide, block, acc, near_tile)
+
+    other_acc = near(False, other_near)
+    own_far = lax.ppermute(own_near, "row", far_route)
+    own_acc = near(True, own_near)
+    sent = call(
+        far_other_kernel, shape((1, tokens_here, half), bf16), [VMEM] * 7, VMEM, work
+    )(wide, other_near, other_far, acc, other_acc, near_tile, far_tile)
+    got = lax.ppermute(sent, "mp", [(0, 1), (1, 0)])
+    outputs, gap = call(
+        far_own_kernel,
+        (
+            shape((1, tokens_here, width), bf16),
+            shape((heads_local // 2, tokens_here), f32),
+        ),
+        [VMEM] * 9,
+        [HBM, VMEM],
+        work,
+        scratch_shapes=[
+            pltpu.VMEM((tokens_here, half), bf16),
+            pltpu.SemaphoreType.DMA((1 + kv_local // 2,)),
+        ],
+    )(wide, own_near, own_far, acc, own_acc, near_tile, far_tile, sent, got)
+    return (outputs, gap)
+
+
+def two_hops(mesh, rollouts):
+    return rollouts == 2 and mesh.shape["row"] // 2 == 2 and mesh.shape["mp"] == 2
+
+
 def solution(mesh):
     in_specs = (
         P("mp", ("groups", "row"), "col"),
@@ -126,6 +467,17 @@
         P("groups"),
     )
     out_specs = (P("mp", ("groups", "row"), "col"), P(("col", "mp"), ("groups", "row")))
-    return jax.shard_map(
-        per_device, mesh=mesh, in_specs=in_specs, out_specs=out_specs, check_vma=False
-    )
+
+    def place(body):
+        return jax.shard_map(
+            body, mesh=mesh, in_specs=in_specs, out_specs=out_specs, check_vma=False
+        )
+
+    def step(queries, keys, values, lengths):
+        rollouts = lengths.shape[0] // mesh.shape["groups"]
+        kv_local = keys.shape[2] // HEAD_DIM // mesh.shape["col"]
+        if not two_hops(mesh, rollouts) or kv_local % 2:
+            return place(per_device_general)(queries, keys, values, lengths)
+        return place(per_device_paired)(queries, keys, values, lengths)
+
+    return step

time: 104 us -> 45.2 us (0.43)
  the two profiles are of different devices: /device:TPU:17 before, /device:TPU:22 now
where the time goes in v2:
time: 45.2 us; the launch traced here: 44.9 us
  waiting for transfers between devices  17.1 us (38%)
  starting transfers between devices  14 us (31%)
  Pallas kernels  10.2 us (23%)
  local copies, waits for them, and re-layouts  2.83 us (6%)
  between operations  0.73 us (2%)
    ppermute x1, waiting for transfers between devices, per_device_paired(): own_near = lax.ppermute(own, 'row', near_route)  7.1 us
    ppermute x1, waiting for transfers between devices, per_device_paired(): own_far = lax.ppermute(own_near, 'row', far_route)  5.12 us
    ppermute x1, waiting for transfers between devices, per_device_paired(): other_near = lax.ppermute(other, 'row', near_route)  4.6 us
    pallas_call x1, Pallas kernels, per_device_paired(): call(diagonal_kernel, (shape((tokens_here, 2 * width), bf16), shape((toke...  4.14 us
    ppermute x1, starting transfers between devices, per_device_paired(): other_near = lax.ppermute(other, 'row', near_route)  3.48 us
    ppermute x1, starting transfers between devices, per_device_paired(): own_near = lax.ppermute(own, 'row', near_route)  3.48 us
    ppermute x1, starting transfers between devices, per_device_paired(): other_far = lax.ppermute(other_near, 'row', far_route)  3.47 us
    ppermute x1, starting transfers between devices, per_device_paired(): own_far = lax.ppermute(own_near, 'row', far_route)  3.47 us
  transfers between devices with their start and end apart: 5, of which 4 were waited for; matrix products, arithmetic and copies ran while one was open for 4% of the time, Pallas kernels for 14%

profile of v2, /device:TPU:22, one launch (start us, length us, event | category | flops | bytes accessed | tf_op | source)
XLA Modules:
  0.0 44.9 jit_solution(4974655667719594521)
XLA Ops:
  0.6 1.0 %constant_dynamic-slice_fusion.2 = (bf16[1,256,256]{2,1,0:T(8,128)(2,1)S(1)}, bf16[1,256,256]{2,1,0:T(8,128)(2,1)S(1)}) fusion(bf16[1,256,512]{2,1,0:T(8,128)(2,1)} %param.6, s32[]{:T(128)S(6)} %select_n.8, bf16[1,256,512]{2,1,0:T(8,128)(2,1)} %param.5), kind=kLoop, calls=%fused_computation.4 | loop fusion | bytes 524292 | tf_op jit(solution)/shard_map/dynamic_slice | solution.py:394
  1.7 3.5 %collective-permute-start.2 = (bf16[2,256,256]{2,1,0:T(8,128)(2,1)S(1)}, bf16[2,256,256]{2,1,0:T(8,128)(2,1)S(1)}, u32[]{:S(2)}, u32[]{:S(2)}) collective-permute-start(bf16[2,256,256]{2,1,0:T(8,128)(2,1)S(1)} %pad_maximum_fusion.other_ref), channel_id=1, source_target_pairs={{0,4},{4,8},{8,12},{1,5},{5,9},{9,13},{2,6},{6,10},{10,14},{3,7},{... | collective-permute-start | bytes 786440 | tf_op jit(solution)/shard_map/ppermute | solution.py:400
  5.2 0.9 %constant_dynamic-slice_fusion = bf16[1,256,256]{2,1,0:T(8,128)(2,1)S(1)} fusion(bf16[1,256,512]{2,1,0:T(8,128)(2,1)} %param.6, s32[]{:T(128)S(6)} %select_n.9), kind=kLoop, calls=%fused_computation.2 | loop fusion | bytes 262148 | tf_op jit(solution)/shard_map/dynamic_slice | solution.py:394
  6.1 0.9 %constant_dynamic-slice_fusion.1 = bf16[1,256,256]{2,1,0:T(8,128)(2,1)S(1)} fusion(bf16[1,256,512]{2,1,0:T(8,128)(2,1)} %param.5, s32[]{:T(128)S(6)} %select_n.9), kind=kLoop, calls=%fused_computation.3 | loop fusion | bytes 262148 | tf_op jit(solution)/shard_map/dynamic_slice | solution.py:394
  7.0 4.6 %collective-permute-done.2.refs_1_ = bf16[2,256,256]{2,1,0:T(8,128)(2,1)S(1)} collective-permute-done((bf16[2,256,256]{2,1,0:T(8,128)(2,1)S(1)}, bf16[2,256,256]{2,1,0:T(8,128)(2,1)S(1)}, u32[]{:S(2)}, u32[]{:S(2)}) %collective-permute-start.2) | collective-permute-done | bytes 262176 | tf_op jit(solution)/shard_map/ppermute | solution.py:400
  11.6 3.5 %collective-permute-start.3 = (bf16[2,256,256]{2,1,0:T(8,128)(2,1)S(1)}, bf16[2,256,256]{2,1,0:T(8,128)(2,1)S(1)}, u32[]{:S(2)}, u32[]{:S(2)}) collective-permute-start(bf16[2,256,256]{2,1,0:T(8,128)(2,1)S(1)} %collective-permute-done.2.refs_1_), channel_id=1, source_target_pairs={{4,8},{8,12},{5,9},{9,13},{6,10},{10,14},{7,11},{11,15},{20,24},{2... | collective-permute-start | bytes 786440 | tf_op jit(solution)/shard_map/ppermute | solution.py:423
  15.1 4.1 %shard_map.59 = (bf16[256,5120]{1,0:T(8,128)(2,1)S(1)}, f32[256,5120]{1,0:T(8,128)S(1)}, bf16[256,128]{1,0:T(8,128)(2,1)S(1)}, bf16[256,128]{1,0:T(8,128)(2,1)S(1)}) custom-call(s32[2]{0:T(128)} %len_hbm.1, bf16[1,256,2560]{2,1,0:T(8,128)(2,1)} %q_hbm.1, bf16[2,256,256]{2,1,0:T(8,128)(2,1)S(1)} %pad_maximum_fusion.other_ref, ...), custom_call_target="tpu_custom_call" | custom-call | flops 1342177280 | bytes 4194304 | tf_op jit(solution)/shard_map/pallas_call | solution.py:404
  19.3 1.1 %shard_map.61.refs_4_ = f32[256,2560]{1,0:T(8,128)S(1)} custom-call(bf16[256,5120]{1,0:T(8,128)(2,1)S(1)} %get-tuple-element.10.refs_0_, bf16[2,256,256]{2,1,0:T(8,128)(2,1)S(1)} %collective-permute-done.2.refs_1_, f32[256,5120]{1,0:T(8,128)S(1)} %get-tuple-element.11.refs_2_.refs_3_, bf16[256,128]{1,0:T(8,128)(2,1)S(1)} %get-tuple-element.12.refs_3_.refs_5_), custom_call_target="tpu_custom_call" | custom-call | flops 1342177280 | bytes 4194304 | tf_op jit(solution)/shard_map/pallas_call | solution.py:426
  20.4 0.3 collective-permute-done.3.refs_2_
  20.7 1.2 %shard_map.62.refs_7_ = bf16[1,256,1280]{2,1,0:T(8,128)(2,1)S(1)} custom-call(bf16[256,5120]{1,0:T(8,128)(2,1)S(1)} %get-tuple-element.10.refs_0_, bf16[2,256,256]{2,1,0:T(8,128)(2,1)S(1)} %collective-permute-done.2.refs_1_, bf16[2,256,256]{2,1,0:T(8,128)(2,1)S(1)} %collective-permute-done.3.refs_2_, f32[256,5120]{1,0:T(8,128)S(1)} %get-tuple-element.11.refs_2_.refs_3_, ...), custom_call_target="tpu_custom_call" | custom-call | flops 1342177280 | bytes 4194304 | tf_op jit(solution)/shard_map/pallas_call | solution.py:437
  21.9 0.1 collective-permute-start.4
  22.0 3.5 %collective-permute-start = (bf16[2,256,256]{2,1,0:T(8,128)(2,1)S(1)}, bf16[2,256,256]{2,1,0:T(8,128)(2,1)S(1)}, u32[]{:S(2)}, u32[]{:S(2)}) collective-permute-start(bf16[2,256,256]{2,1,0:T(8,128)(2,1)S(1)} %pad_maximum_fusion.1.own_ref), channel_id=1, source_target_pairs={{0,4},{4,8},{8,12},{1,5},{5,9},{9,13},{2,6},{6,10},{10,14},{3,7},{... | collective-permute-start | bytes 786440 | tf_op jit(solution)/shard_map/ppermute | solution.py:403
  25.5 7.1 %collective-permute-done.refs_1_ = bf16[2,256,256]{2,1,0:T(8,128)(2,1)S(1)} collective-permute-done((bf16[2,256,256]{2,1,0:T(8,128)(2,1)S(1)}, bf16[2,256,256]{2,1,0:T(8,128)(2,1)S(1)}, u32[]{:S(2)}, u32[]{:S(2)}) %collective-permute-start) | collective-permute-done | bytes 262176 | tf_op jit(solution)/shard_map/ppermute | solution.py:403
  32.6 3.5 %collective-permute-start.1 = (bf16[2,256,256]{2,1,0:T(8,128)(2,1)S(1)}, bf16[2,256,256]{2,1,0:T(8,128)(2,1)S(1)}, u32[]{:S(2)}, u32[]{:S(2)}) collective-permute-start(bf16[2,256,256]{2,1,0:T(8,128)(2,1)S(1)} %collective-permute-done.refs_1_), channel_id=1, source_target_pairs={{4,8},{8,12},{5,9},{9,13},{6,10},{10,14},{7,11},{11,15},{20,24},{2... | collective-permute-start | bytes 786440 | tf_op jit(solution)/shard_map/ppermute | solution.py:435
  36.1 1.1 %shard_map.60.refs_4_ = f32[256,2560]{1,0:T(8,128)S(1)} custom-call(bf16[256,5120]{1,0:T(8,128)(2,1)S(1)} %get-tuple-element.10.refs_0_, bf16[2,256,256]{2,1,0:T(8,128)(2,1)S(1)} %collective-permute-done.refs_1_, f32[256,5120]{1,0:T(8,128)S(1)} %get-tuple-element.11.refs_2_.refs_3_, bf16[256,128]{1,0:T(8,128)(2,1)S(1)} %get-tuple-element.12.refs_3_.refs_5_), custom_call_target="tpu_custom_call" | custom-call | flops 1342177280 | bytes 4194304 | tf_op jit(solution)/shard_map/pallas_call | solution.py:426
  37.2 5.1 %collective-permute-done.1.refs_2_ = bf16[2,256,256]{2,1,0:T(8,128)(2,1)S(1)} collective-permute-done((bf16[2,256,256]{2,1,0:T(8,128)(2,1)S(1)}, bf16[2,256,256]{2,1,0:T(8,128)(2,1)S(1)}, u32[]{:S(2)}, u32[]{:S(2)}) %collective-permute-start.1) | collective-permute-done | bytes 262176 | tf_op jit(solution)/shard_map/ppermute | solution.py:435
  42.3 0.0 collective-permute-done.4.refs_8_
  42.3 2.6 %shard_map.63 = (bf16[1,256,2560]{2,1,0:T(8,128)(2,1)}, f32[10,256]{1,0:T(8,128)}) custom-call(bf16[256,5120]{1,0:T(8,128)(2,1)S(1)} %get-tuple-element.10.refs_0_, bf16[2,256,256]{2,1,0:T(8,128)(2,1)S(1)} %collective-permute-done.refs_1_, bf16[2,256,256]{2,1,0:T(8,128)(2,1)S(1)} %collective-permute-done.1.refs_2_, ...), custom_call_target="tpu_custom_call" | custom-call | flops 1342177280 | bytes 4194304 | tf_op jit(solution)/shard_map/pallas_call | solution.py:441
  (2 shorter events, 0.1 us)
Async XLA Ops:
  1.7 9.9 %collective-permute-start.2 = (bf16[2,256,256]{2,1,0:T(8,128)(2,1)S(1)}, bf16[2,256,256]{2,1,0:T(8,128)(2,1)S(1)}, u32[]{:S(2)}, u32[]{:S(2)}) collective-permute-start(bf16[2,256,256]{2,1,0:T(8,128)(2,1)S(1)} %pad_maximum_fusion.other_ref), channel_id=1, source_target_pairs={{0,4},{4,8},{8,12},{1,5},{5,9},{9,13},{2,6},{6,10},{10,14},{3,7},{... | collective-permute-start | bytes 786440 | tf_op jit(solution)/shard_map/ppermute | solution.py:400
  11.6 9.1 %collective-permute-start.3 = (bf16[2,256,256]{2,1,0:T(8,128)(2,1)S(1)}, bf16[2,256,256]{2,1,0:T(8,128)(2,1)S(1)}, u32[]{:S(2)}, u32[]{:S(2)}) collective-permute-start(bf16[2,256,256]{2,1,0:T(8,128)(2,1)S(1)} %collective-permute-done.2.refs_1_), channel_id=1, source_target_pairs={{4,8},{8,12},{5,9},{9,13},{6,10},{10,14},{7,11},{11,15},{20,24},{2... | collective-permute-start | bytes 786440 | tf_op jit(solution)/shard_map/ppermute | solution.py:423
  21.9 20.4 %collective-permute-start.4 = (bf16[1,256,1280]{2,1,0:T(8,128)(2,1)S(1)}, bf16[1,256,1280]{2,1,0:T(8,128)(2,1)S(1)}, u32[]{:S(2)}, u32[]{:S(2)}) collective-permute-start(bf16[1,256,1280]{2,1,0:T(8,128)(2,1)S(1)} %shard_map.62.refs_7_), channel_id=1, source_target_pairs={{0,1},{1,0},{2,3},{3,2},{4,5},{5,4},{6,7},{7,6},{8,9},{9,8},{10,11... | collective-permute-start | bytes 1966088 | tf_op jit(solution)/shard_map/ppermute | solution.py:440
  22.0 10.6 %collective-permute-start = (bf16[2,256,256]{2,1,0:T(8,128)(2,1)S(1)}, bf16[2,256,256]{2,1,0:T(8,128)(2,1)S(1)}, u32[]{:S(2)}, u32[]{:S(2)}) collective-permute-start(bf16[2,256,256]{2,1,0:T(8,128)(2,1)S(1)} %pad_maximum_fusion.1.own_ref), channel_id=1, source_target_pairs={{0,4},{4,8},{8,12},{1,5},{5,9},{9,13},{2,6},{6,10},{10,14},{3,7},{... | collective-permute-start | bytes 786440 | tf_op jit(solution)/shard_map/ppermute | solution.py:403
  32.6 9.7 %collective-permute-start.1 = (bf16[2,256,256]{2,1,0:T(8,128)(2,1)S(1)}, bf16[2,256,256]{2,1,0:T(8,128)(2,1)S(1)}, u32[]{:S(2)}, u32[]{:S(2)}) collective-permute-start(bf16[2,256,256]{2,1,0:T(8,128)(2,1)S(1)} %collective-permute-done.refs_1_), channel_id=1, source_target_pairs={{4,8},{8,12},{5,9},{9,13},{6,10},{10,14},{7,11},{11,15},{20,24},{2... | collective-permute-start | bytes 786440 | tf_op jit(solution)/shard_map/ppermute | solution.py:435

commit v3 on v2

--- a/solution.py
+++ b/solution.py
@@ -124,6 +124,7 @@
 GROUP = HEADS // KV_HEADS
 BIG = 2.0**100
 LIMIT = 2.0**100
+PIECES = 4
 NT = (((1,), (1,)), ((), ()))
 VMEM = pl.BlockSpec(memory_space=pltpu.VMEM)
 SMEM = pl.BlockSpec(memory_space=pltpu.SMEM)
@@ -160,29 +161,60 @@
     return tile
 
 
+def column_copies(source, target, sems, pieces):
+    rows = target.shape[0] // pieces
+    return [
+        pltpu.make_async_copy(
+            source.at[pl.ds(piece * rows, rows)], target.at[pl.ds(piece * rows, rows)], sems[piece]
+        )
+        for piece in range(pieces)
+    ]
+
+
+def run_all(copies):
+    for copy in copies:
+        copy.start()
+    for copy in copies:
+        copy.wait()
+
+
+def pack_copies(which, k_hbm, v_hbm, pack_ref, sem):
+    width = pack_ref.shape[2]
+    copies = []
+    for index, ref in enumerate((k_hbm, v_hbm)):
+        sems = [sem.at[index * PIECES + piece] for piece in range(PIECES)]
+        copies += column_copies(ref.at[0, :, lanes(which, width)], pack_ref.at[index], sems, PIECES)
+    return copies
+
+
+def pack_kernel(k_hbm, v_hbm, pack_ref, sem):
+    run_all(pack_copies(1 - lax.axis_index("mp"), k_hbm, v_hbm, pack_ref, sem))
+
+
+def load_kernel(k_hbm, v_hbm, q_hbm, after_ref, pack_ref, q_ref, sem):
+    del after_ref
+    mp = lax.axis_index("mp")
+    width = q_ref.shape[1] // 2
+    copies = pack_copies(mp, k_hbm, v_hbm, pack_ref, sem)
+    for index, which in enumerate((1 - mp, mp)):
+        copies += column_copies(
+            q_hbm.at[0, :, lanes(which, width)],
+            q_ref.at[:, lanes(index, width)],
+            [sem.at[2 * PIECES + index]],
+            1,
+        )
+    run_all(copies)
+
+
 def diagonal_kernel(
-    len_hbm, q_hbm, other_ref, own_ref, wide_ref, acc_ref, near_ref, far_ref, bias_ref, q_ref,
-    len_ref, sem
+    len_hbm, q_ref, other_ref, own_ref, wide_ref, acc_ref, near_ref, far_ref, bias_ref, len_ref, sem
 ):
     tokens_here = q_ref.shape[0]
     half = tokens_here // 2
-    mp = lax.axis_index("mp")
     row_pos = lax.axis_index("row")
     kv_half = other_ref.shape[2] // HEAD_DIM
-    spot = GROUP * HEAD_DIM
-    len_copy = pltpu.make_async_copy(len_hbm, len_ref, sem.at[2 * kv_half])
+    len_copy = pltpu.make_async_copy(len_hbm, len_ref, sem.at[0])
     len_copy.start()
-    copies = []
-    for step in range(2 * kv_half):
-        which = 1 - mp if step < kv_half else mp
-        copies.append(
-            pltpu.make_async_copy(
-                q_hbm.at[0, :, lanes(which * kv_half + step % kv_half, spot)],
-                q_ref.at[:, lanes(step, spot)],
-                sem.at[step],
-            )
-        )
-        copies[step].start()
     len_copy.wait()
     boundary = len_ref[0] - row_pos * tokens_here
     query = lax.broadcasted_iota(jnp.int32, (tokens_here, tokens_here), 0)
@@ -198,7 +230,6 @@
     later = in_columns(tile, 0.0, jnp.where(token >= boundary, 1.0, 0.0), 1.0)
     first_lane = lax.broadcasted_iota(jnp.int32, (half, HEAD_DIM), 1) == 0
     for step in range(2 * kv_half):
-        copies[step].wait()
         pack_ref = other_ref if step < kv_half else own_ref
         key_rows = pack_ref[0, :, lanes(step % kv_half, HEAD_DIM)]
         value_rows = value_of(pack_ref, step % kv_half)
@@ -289,26 +320,25 @@
 
 
 def far_own_kernel(*refs):
-    refs, (sent_ref, got_ref, out_ref, gap_ref, mine_ref, sem) = refs[:7], refs[7:]
+    refs, (sent_ref, got_ref, out_ref, gap_out, mine_ref, gap_ref, sem) = refs[:7], refs[7:]
     width = sent_ref.shape[2]
     tokens_here = sent_ref.shape[1]
     heads_half = width // HEAD_DIM
     mp = lax.axis_index("mp")
     first_head = heads_half
-    spot = GROUP * HEAD_DIM
-    steps = heads_half // GROUP
     sent_copy = pltpu.make_async_copy(
-        sent_ref.at[0], out_ref.at[0, :, lanes(1 - mp, width)], sem.at[steps]
+        sent_ref.at[0], out_ref.at[0, :, lanes(1 - mp, width)], sem.at[heads_half]
     )
     sent_copy.start()
-    mine_copies = [
-        pltpu.make_async_copy(
-            mine_ref.at[:, lanes(step, spot)],
-            out_ref.at[0, :, lanes(mp * steps + step, spot)],
-            sem.at[step],
-        )
-        for step in range(steps)
-    ]
+    gap_copy = pltpu.make_async_copy(gap_ref, gap_out, sem.at[heads_half + 1])
+
+    def mine_copy(local):
+        return pltpu.make_async_copy(
+            mine_ref.at[:, lanes(local, HEAD_DIM)],
+            out_ref.at[0, :, lanes(mp * heads_half + local, HEAD_DIM)],
+            sem.at[local],
+        )
+
     lane = lax.broadcasted_iota(jnp.int32, (tokens_here, HEAD_DIM), 1)
     state = {"far": jnp.zeros((tokens_here, HEAD_DIM), jnp.float32)}
     state["size"] = state["far"]
@@ -328,17 +358,18 @@
 
     def store(local, block):
         mine_ref[:, lanes(local, HEAD_DIM)] = block
-        if local % GROUP == GROUP - 1:
-            mine_copies[local // GROUP].start()
+        mine_copy(local).start()
         far, size = squares(local, block)
         state["far"] = jnp.where(lane == local, far, state["far"])
         state["size"] = jnp.where(lane == local, size, state["size"])
 
     too_high = far_heads(first_head, refs, store)
     gap_ref[...] = gap_of(state["far"], state["size"])
+    gap_copy.start()
     sent_copy.wait()
-    for copy in mine_copies:
-        copy.wait()
+    for local in range(heads_half):
+        mine_copy(local).wait()
+    gap_copy.wait()
 
     @pl.when(too_high)
     def _():
@@ -351,11 +382,12 @@
             parts = squares(local, mine_ref[:, lanes(local, HEAD_DIM)])
             far = jnp.where(lane == local, parts[0], far)
             size = jnp.where(lane == local, parts[1], size)
+            mine_copy(local).start()
         gap_ref[...] = gap_of(far, size)
-        for copy in mine_copies:
-            copy.start()
-        for copy in mine_copies:
-            copy.wait()
+        gap_copy.start()
+        for local in range(heads_half):
+            mine_copy(local).wait()
+        gap_copy.wait()
 
 
 def in_hbm(array):
@@ -384,22 +416,31 @@
     half = width // 2
     half_kv = keys.shape[2] // 2
     count = lax.axis_size("row")
-    mp = lax.axis_index("mp")
     f32, bf16 = jnp.float32, jnp.bfloat16
     shape = jax.ShapeDtypeStruct
     tile_type = shape((tokens_here, HEAD_DIM), bf16)
     work = 8 * heads_local * tokens_here * tokens_here * HEAD_DIM
 
-    def pack(which):
-        parts = [lax.dynamic_slice_in_dim(x, which * half_kv, half_kv, 2) for x in (keys, values)]
-        return jnp.concatenate(parts, axis=0)
-
     near_route = [(i - 1, i) for i in range(1, count)]
     far_route = [(i - 1, i) for i in range(2, count)]
-    other = pack(1 - mp)
+    pack_type = shape((2, tokens_here, half_kv), bf16)
+    other = call(
+        pack_kernel,
+        pack_type,
+        [HBM] * 2,
+        VMEM,
+        work,
+        scratch_shapes=[pltpu.SemaphoreType.DMA((2 * PIECES,))],
+    )(in_hbm(keys), in_hbm(values))
     other_near = lax.ppermute(other, "row", near_route)
-    other, which = lax.optimization_barrier((other, mp))
-    own = pack(which)
+    own, query_rows = call(
+        load_kernel,
+        (pack_type, shape((tokens_here, width), bf16)),
+        [HBM] * 4,
+        [VMEM] * 2,
+        work,
+        scratch_shapes=[pltpu.SemaphoreType.DMA((2 * PIECES + 2,))],
+    )(in_hbm(keys), in_hbm(values), in_hbm(queries), other)
     own_near = lax.ppermute(own, "row", near_route)
     wide, acc, near_tile, far_tile = call(
         diagonal_kernel,
@@ -409,17 +450,16 @@
             tile_type,
             tile_type,
         ),
-        [HBM] * 2 + [VMEM] * 2,
+        [HBM] + [VMEM] * 3,
         [VMEM] * 4,
         work,
         vmem_mib=16,
         scratch_shapes=[
             pltpu.VMEM((tokens_here, tokens_here), f32),
-            pltpu.VMEM((tokens_here, width), bf16),
             pltpu.SMEM(lengths.shape, jnp.int32),
-            pltpu.SemaphoreType.DMA((1 + kv_local,)),
+            pltpu.SemaphoreType.DMA((1,)),
         ],
-    )(in_hbm(lengths), in_hbm(queries), other, own)
+    )(in_hbm(lengths), query_rows, other, own)
     other_far = lax.ppermute(other_near, "row", far_route)
 
     def near(own, block):
@@ -445,11 +485,12 @@
             shape((heads_local // 2, tokens_here), f32),
         ),
         [VMEM] * 9,
-        [HBM, VMEM],
+        [HBM, HBM],
         work,
         scratch_shapes=[
             pltpu.VMEM((tokens_here, half), bf16),
-            pltpu.SemaphoreType.DMA((1 + kv_local // 2,)),
+            pltpu.VMEM((heads_local // 2, tokens_here), f32),
+            pltpu.SemaphoreType.DMA((2 + heads_local // 2,)),
         ],
     )(wide, own_near, own_far, acc, own_acc, near_tile, far_tile, sent, got)
     return (outputs, gap)

time: 45.2 us -> 44.7 us (0.989)
  the two profiles are of different devices: /device:TPU:22 before, /device:TPU:16 now
where the time goes in v3:
time: 44.7 us; the launch traced here: 44.4 us
  waiting for transfers between devices  18.8 us (42%)
  starting transfers between devices  14 us (31%)
  Pallas kernels  10.8 us (24%)
  between operations  0.72 us (2%)
    ppermute x1, waiting for transfers between devices, per_device_paired(): own_near = lax.ppermute(own, 'row', near_route)  7.1 us
    ppermute x1, waiting for transfers between devices, per_device_paired(): other_near = lax.ppermute(other, 'row', near_route)  6.45 us
    ppermute x1, waiting for transfers between devices, per_device_paired(): own_far = lax.ppermute(own_near, 'row', far_route)  5.12 us
    ppermute x1, starting transfers between devices, per_device_paired(): own_near = lax.ppermute(own, 'row', near_route)  3.49 us
    ppermute x1, starting transfers between devices, per_device_paired(): other_near = lax.ppermute(other, 'row', near_route)  3.48 us
    ppermute x1, starting transfers between devices, per_device_paired(): own_far = lax.ppermute(own_near, 'row', far_route)  3.47 us
    ppermute x1, starting transfers between devices, per_device_paired(): other_far = lax.ppermute(other_near, 'row', far_route)  3.47 us
    pallas_call x1, Pallas kernels, per_device_paired(): call(diagonal_kernel, (shape((tokens_here, 2 * width), bf16), shape((toke...  2.74 us
  transfers between devices with their start and end apart: 5, of which 4 were waited for; matrix products, arithmetic and copies ran while one was open for 0% of the time, Pallas kernels for 15%

profile of v3, /device:TPU:16, one launch (start us, length us, event | category | flops | bytes accessed | tf_op | source)
XLA Modules:
  0.0 44.4 jit_solution(10469574694837932118)
XLA Ops:
  0.6 1.0 %shard_map.59.after_ref.other_ref = bf16[2,256,256]{2,1,0:T(8,128)(2,1)S(1)} custom-call(bf16[1,256,512]{2,1,0:T(8,128)(2,1)} %k_hbm.3, bf16[1,256,512]{2,1,0:T(8,128)(2,1)} %v_hbm.3), custom_call_target="tpu_custom_call" | custom-call | flops 1342177280 | bytes 4194304 | tf_op jit(solution)/shard_map/pallas_call | solution.py:427
  1.6 3.5 %collective-permute-start.2 = (bf16[2,256,256]{2,1,0:T(8,128)(2,1)S(1)}, bf16[2,256,256]{2,1,0:T(8,128)(2,1)S(1)}, u32[]{:S(2)}, u32[]{:S(2)}) collective-permute-start(bf16[2,256,256]{2,1,0:T(8,128)(2,1)S(1)} %shard_map.59.after_ref.other_ref), channel_id=1, source_target_pairs={{0,4},{4,8},{8,12},{1,5},{5,9},{9,13},{2,6},{6,10},{10,14},{3,7},{... | collective-permute-start | bytes 786440 | tf_op jit(solution)/shard_map/ppermute | solution.py:435
  5.1 6.4 %collective-permute-done.2.refs_1_ = bf16[2,256,256]{2,1,0:T(8,128)(2,1)S(1)} collective-permute-done((bf16[2,256,256]{2,1,0:T(8,128)(2,1)S(1)}, bf16[2,256,256]{2,1,0:T(8,128)(2,1)S(1)}, u32[]{:S(2)}, u32[]{:S(2)}) %collective-permute-start.2) | collective-permute-done | bytes 262176 | tf_op jit(solution)/shard_map/ppermute | solution.py:435
  11.5 3.5 %collective-permute-start.3 = (bf16[2,256,256]{2,1,0:T(8,128)(2,1)S(1)}, bf16[2,256,256]{2,1,0:T(8,128)(2,1)S(1)}, u32[]{:S(2)}, u32[]{:S(2)}) collective-permute-start(bf16[2,256,256]{2,1,0:T(8,128)(2,1)S(1)} %collective-permute-done.2.refs_1_), channel_id=1, source_target_pairs={{4,8},{8,12},{5,9},{9,13},{6,10},{10,14},{7,11},{11,15},{20,24},{2... | collective-permute-start | bytes 786440 | tf_op jit(solution)/shard_map/ppermute | solution.py:463
  15.0 1.5 %shard_map.60 = (bf16[2,256,256]{2,1,0:T(8,128)(2,1)S(1)}, bf16[256,2560]{1,0:T(8,128)(2,1)S(1)}) custom-call(bf16[1,256,512]{2,1,0:T(8,128)(2,1)} %k_hbm.3, bf16[1,256,512]{2,1,0:T(8,128)(2,1)} %v_hbm.3, bf16[1,256,2560]{2,1,0:T(8,128)(2,1)} %q_hbm.1, bf16[2,256,256]{2,1,0:T(8,128)(2,1)S(1)} %shard_map.59.after_ref.other_ref), custom_call_target="tpu_custom_call" | custom-call | flops 1342177280 | bytes 4194304 | tf_op jit(solution)/shard_map/pallas_call | solution.py:436
  16.6 2.7 %shard_map.61 = (bf16[256,5120]{1,0:T(8,128)(2,1)S(1)}, f32[256,5120]{1,0:T(8,128)S(1)}, bf16[256,128]{1,0:T(8,128)(2,1)S(1)}, bf16[256,128]{1,0:T(8,128)(2,1)S(1)}) custom-call(s32[2]{0:T(128)} %len_hbm.1, bf16[256,2560]{1,0:T(8,128)(2,1)S(1)} %get-tuple-element.8.q_ref, bf16[2,256,256]{2,1,0:T(8,128)(2,1)S(1)} %shard_map.59.after_ref.other_ref, ...), custom_call_target="tpu_custom_call" | custom-call | flops 1342177280 | bytes 4194304 | tf_op jit(solution)/shard_map/pallas_call | solution.py:445
  19.3 1.1 %shard_map.63.refs_4_ = f32[256,2560]{1,0:T(8,128)S(1)} custom-call(bf16[256,5120]{1,0:T(8,128)(2,1)S(1)} %get-tuple-element.10.refs_0_, bf16[2,256,256]{2,1,0:T(8,128)(2,1)S(1)} %collective-permute-done.2.refs_1_, f32[256,5120]{1,0:T(8,128)S(1)} %get-tuple-element.11.refs_2_.refs_3_, bf16[256,128]{1,0:T(8,128)(2,1)S(1)} %get-tuple-element.12.refs_3_.refs_5_), custom_call_target="tpu_custom_call" | custom-call | flops 1342177280 | bytes 4194304 | tf_op jit(solution)/shard_map/pallas_call | solution.py:466
  20.4 0.2 collective-permute-done.3.refs_2_
  20.6 1.2 %shard_map.64.refs_7_ = bf16[1,256,1280]{2,1,0:T(8,128)(2,1)S(1)} custom-call(bf16[256,5120]{1,0:T(8,128)(2,1)S(1)} %get-tuple-element.10.refs_0_, bf16[2,256,256]{2,1,0:T(8,128)(2,1)S(1)} %collective-permute-done.2.refs_1_, bf16[2,256,256]{2,1,0:T(8,128)(2,1)S(1)} %collective-permute-done.3.refs_2_, f32[256,5120]{1,0:T(8,128)S(1)} %get-tuple-element.11.refs_2_.refs_3_, ...), custom_call_target="tpu_custom_call" | custom-call | flops 1342177280 | bytes 4194304 | tf_op jit(solution)/shard_map/pallas_call | solution.py:477
  21.8 0.1 collective-permute-start.4
  21.9 3.5 %collective-permute-start = (bf16[2,256,256]{2,1,0:T(8,128)(2,1)S(1)}, bf16[2,256,256]{2,1,0:T(8,128)(2,1)S(1)}, u32[]{:S(2)}, u32[]{:S(2)}) collective-permute-start(bf16[2,256,256]{2,1,0:T(8,128)(2,1)S(1)} %get-tuple-element.9.own_ref), channel_id=1, source_target_pairs={{0,4},{4,8},{8,12},{1,5},{5,9},{9,13},{2,6},{6,10},{10,14},{3,7},{... | collective-permute-start | bytes 786440 | tf_op jit(solution)/shard_map/ppermute | solution.py:444
  25.4 7.1 %collective-permute-done.refs_1_ = bf16[2,256,256]{2,1,0:T(8,128)(2,1)S(1)} collective-permute-done((bf16[2,256,256]{2,1,0:T(8,128)(2,1)S(1)}, bf16[2,256,256]{2,1,0:T(8,128)(2,1)S(1)}, u32[]{:S(2)}, u32[]{:S(2)}) %collective-permute-start) | collective-permute-done | bytes 262176 | tf_op jit(solution)/shard_map/ppermute | solution.py:444
  32.5 3.5 %collective-permute-start.1 = (bf16[2,256,256]{2,1,0:T(8,128)(2,1)S(1)}, bf16[2,256,256]{2,1,0:T(8,128)(2,1)S(1)}, u32[]{:S(2)}, u32[]{:S(2)}) collective-permute-start(bf16[2,256,256]{2,1,0:T(8,128)(2,1)S(1)} %collective-permute-done.refs_1_), channel_id=1, source_target_pairs={{4,8},{8,12},{5,9},{9,13},{6,10},{10,14},{7,11},{11,15},{20,24},{2... | collective-permute-start | bytes 786440 | tf_op jit(solution)/shard_map/ppermute | solution.py:475
  36.0 1.1 %shard_map.62.refs_4_ = f32[256,2560]{1,0:T(8,128)S(1)} custom-call(bf16[256,5120]{1,0:T(8,128)(2,1)S(1)} %get-tuple-element.10.refs_0_, bf16[2,256,256]{2,1,0:T(8,128)(2,1)S(1)} %collective-permute-done.refs_1_, f32[256,5120]{1,0:T(8,128)S(1)} %get-tuple-element.11.refs_2_.refs_3_, bf16[256,128]{1,0:T(8,128)(2,1)S(1)} %get-tuple-element.12.refs_3_.refs_5_), custom_call_target="tpu_custom_call" | custom-call | flops 1342177280 | bytes 4194304 | tf_op jit(solution)/shard_map/pallas_call | solution.py:466
  37.1 5.1 %collective-permute-done.1.refs_2_ = bf16[2,256,256]{2,1,0:T(8,128)(2,1)S(1)} collective-permute-done((bf16[2,256,256]{2,1,0:T(8,128)(2,1)S(1)}, bf16[2,256,256]{2,1,0:T(8,128)(2,1)S(1)}, u32[]{:S(2)}, u32[]{:S(2)}) %collective-permute-start.1) | collective-permute-done | bytes 262176 | tf_op jit(solution)/shard_map/ppermute | solution.py:475
  42.2 0.0 collective-permute-done.4.refs_8_
  42.2 2.1 %shard_map.65 = (bf16[1,256,2560]{2,1,0:T(8,128)(2,1)}, f32[10,256]{1,0:T(8,128)}) custom-call(bf16[256,5120]{1,0:T(8,128)(2,1)S(1)} %get-tuple-element.10.refs_0_, bf16[2,256,256]{2,1,0:T(8,128)(2,1)S(1)} %collective-permute-done.refs_1_, bf16[2,256,256]{2,1,0:T(8,128)(2,1)S(1)} %collective-permute-done.1.refs_2_, ...), custom_call_target="tpu_custom_call" | custom-call | flops 1342177280 | bytes 4194304 | tf_op jit(solution)/shard_map/pallas_call | solution.py:481
Async XLA Ops:
  1.6 9.9 %collective-permute-start.2 = (bf16[2,256,256]{2,1,0:T(8,128)(2,1)S(1)}, bf16[2,256,256]{2,1,0:T(8,128)(2,1)S(1)}, u32[]{:S(2)}, u32[]{:S(2)}) collective-permute-start(bf16[2,256,256]{2,1,0:T(8,128)(2,1)S(1)} %shard_map.59.after_ref.other_ref), channel_id=1, source_target_pairs={{0,4},{4,8},{8,12},{1,5},{5,9},{9,13},{2,6},{6,10},{10,14},{3,7},{... | collective-permute-start | bytes 786440 | tf_op jit(solution)/shard_map/ppermute | solution.py:435
  11.5 9.1 %collective-permute-start.3 = (bf16[2,256,256]{2,1,0:T(8,128)(2,1)S(1)}, bf16[2,256,256]{2,1,0:T(8,128)(2,1)S(1)}, u32[]{:S(2)}, u32[]{:S(2)}) collective-permute-start(bf16[2,256,256]{2,1,0:T(8,128)(2,1)S(1)} %collective-permute-done.2.refs_1_), channel_id=1, source_target_pairs={{4,8},{8,12},{5,9},{9,13},{6,10},{10,14},{7,11},{11,15},{20,24},{2... | collective-permute-start | bytes 786440 | tf_op jit(solution)/shard_map/ppermute | solution.py:463
  21.8 20.4 %collective-permute-start.4 = (bf16[1,256,1280]{2,1,0:T(8,128)(2,1)S(1)}, bf16[1,256,1280]{2,1,0:T(8,128)(2,1)S(1)}, u32[]{:S(2)}, u32[]{:S(2)}) collective-permute-start(bf16[1,256,1280]{2,1,0:T(8,128)(2,1)S(1)} %shard_map.64.refs_7_), channel_id=1, source_target_pairs={{0,1},{1,0},{2,3},{3,2},{4,5},{5,4},{6,7},{7,6},{8,9},{9,8},{10,11... | collective-permute-start | bytes 1966088 | tf_op jit(solution)/shard_map/ppermute | solution.py:480
  21.9 10.6 %collective-permute-start = (bf16[2,256,256]{2,1,0:T(8,128)(2,1)S(1)}, bf16[2,256,256]{2,1,0:T(8,128)(2,1)S(1)}, u32[]{:S(2)}, u32[]{:S(2)}) collective-permute-start(bf16[2,256,256]{2,1,0:T(8,128)(2,1)S(1)} %get-tuple-element.9.own_ref), channel_id=1, source_target_pairs={{0,4},{4,8},{8,12},{1,5},{5,9},{9,13},{2,6},{6,10},{10,14},{3,7},{... | collective-permute-start | bytes 786440 | tf_op jit(solution)/shard_map/ppermute | solution.py:444
  32.5 9.7 %collective-permute-start.1 = (bf16[2,256,256]{2,1,0:T(8,128)(2,1)S(1)}, bf16[2,256,256]{2,1,0:T(8,128)(2,1)S(1)}, u32[]{:S(2)}, u32[]{:S(2)}) collective-permute-start(bf16[2,256,256]{2,1,0:T(8,128)(2,1)S(1)} %collective-permute-done.refs_1_), channel_id=1, source_target_pairs={{4,8},{8,12},{5,9},{9,13},{6,10},{10,14},{7,11},{11,15},{20,24},{2... | collective-permute-start | bytes 786440 | tf_op jit(solution)/shard_map/ppermute | solution.py:475

commit v4 on v3

--- a/solution.py
+++ b/solution.py
@@ -149,8 +149,8 @@
     return jnp.exp2(scores * SCALE).astype(jnp.bfloat16)
 
 
-def spread(mass, value_rows):
-    return jnp.dot(mass, value_rows, preferred_element_type=jnp.float32)
+def product(left, right):
+    return jnp.dot(left, right, preferred_element_type=jnp.float32)
 
 
 def in_columns(shape, *columns):
@@ -226,7 +226,7 @@
     for hops, ref in ((1, near_ref), (2, far_ref)):
         gone = jnp.where(row_pos >= hops, 0.0, -BIG)
         before = jnp.where(token - hops * tokens_here < boundary, -BIG, 0.0)
-        ref[...] = in_columns(tile, -1.0, before, gone).astype(jnp.bfloat16)
+        ref[...] = in_columns(tile, -1.0, before, gone).T.astype(jnp.bfloat16)
     later = in_columns(tile, 0.0, jnp.where(token >= boundary, 1.0, 0.0), 1.0)
     first_lane = lax.broadcasted_iota(jnp.int32, (half, HEAD_DIM), 1) == 0
     for step in range(2 * kv_half):
@@ -242,81 +242,84 @@
                 scores = scores_of(query_rows, key_rows[:seen]) + bias_ref[rows, :seen]
                 top = jnp.max(scores, axis=1, keepdims=True).astype(jnp.bfloat16)
                 top = top.astype(jnp.float32)
-                acc_ref[rows, lanes(local, 2 * HEAD_DIM)] = spread(
-                    mass_of(scores - top), value_rows[:seen]
-                )
+                spot = pl.ds(local * tokens_here + low, half)
+                acc_ref[spot, :] = product(mass_of(scores - top), value_rows[:seen])
                 extra = jnp.where(first_lane, top, later[low:seen]).astype(jnp.bfloat16)
-                wide_ref[rows, lanes(2 * local, HEAD_DIM)] = query_rows
-                wide_ref[rows, lanes(2 * local + 1, HEAD_DIM)] = extra
+                wide_ref[spot, :] = jnp.concatenate([query_rows, extra], axis=1)
 
 
 def key_of(kv_ref, kv, tile_ref):
-    return jnp.concatenate([kv_ref[0, :, lanes(kv, HEAD_DIM)], tile_ref[...]], axis=1)
+    return jnp.concatenate([kv_ref[0, :, lanes(kv, HEAD_DIM)].T, tile_ref[...]], axis=0)
 
 
 def value_of(kv_ref, kv):
     return with_ones(kv_ref[1, :, lanes(kv, HEAD_DIM)])
 
 
+def group_rows(tokens_here, group):
+    return pl.ds(group * GROUP * tokens_here, GROUP * tokens_here)
+
+
 def near_kernel(own, wide_ref, kv_ref, acc_in, tile_ref, acc_ref):
-    heads_half = acc_ref.shape[1] // (2 * HEAD_DIM)
-    first_head = heads_half if own else 0
-    for local in range(heads_half):
-        if local % GROUP == 0:
-            key_rows = key_of(kv_ref, local // GROUP, tile_ref)
-            value_rows = value_of(kv_ref, local // GROUP)
-        cols = lanes(first_head + local, 2 * HEAD_DIM)
-        mass = mass_of(scores_of(wide_ref[:, cols], key_rows))
-        acc_ref[:, lanes(local, 2 * HEAD_DIM)] = acc_in[:, cols] + spread(mass, value_rows)
-
-
-def far_heads(first_head, refs, store):
+    tokens_here = tile_ref.shape[1]
+    kv_half = acc_ref.shape[0] // (GROUP * tokens_here)
+    for kv in range(kv_half):
+        rows = group_rows(tokens_here, kv + (kv_half if own else 0))
+        mass = mass_of(product(wide_ref[rows, :], key_of(kv_ref, kv, tile_ref)))
+        acc_ref[group_rows(tokens_here, kv), :] = acc_in[rows, :] + product(
+            mass, value_of(kv_ref, kv)
+        )
+
+
+def far_heads(first_group, refs, store):
     wide_ref, _, far_kv, _, acc_ref, _, far_tile = refs
+    tokens_here = far_tile.shape[1]
     worst = None
-    for local in range(acc_ref.shape[1] // (2 * HEAD_DIM)):
-        if local % GROUP == 0:
-            key_rows = key_of(far_kv, local // GROUP, far_tile)
-            value_rows = value_of(far_kv, local // GROUP)
-        mass = mass_of(scores_of(wide_ref[:, lanes(first_head + local, 2 * HEAD_DIM)], key_rows))
-        acc = acc_ref[:, lanes(local, 2 * HEAD_DIM)] + spread(mass, value_rows)
-        total = acc[:, HEAD_DIM:]
-        store(local, (acc[:, :HEAD_DIM] / total).astype(jnp.bfloat16))
-        worst = total if worst is None else jnp.maximum(worst, total)
+    for kv in range(acc_ref.shape[0] // (GROUP * tokens_here)):
+        rows = group_rows(tokens_here, first_group + kv)
+        mass = mass_of(product(wide_ref[rows, :], key_of(far_kv, kv, far_tile)))
+        acc = acc_ref[group_rows(tokens_here, kv), :] + product(mass, value_of(far_kv, kv))
+        for g in range(GROUP):
+            part = acc[g * tokens_here : (g + 1) * tokens_here]
+            total = part[:, HEAD_DIM:]
+            store(kv * GROUP + g, (part[:, :HEAD_DIM] / total).astype(jnp.bfloat16))
+            worst = total if worst is None else jnp.maximum(worst, total)
     return jnp.logical_not(jnp.max(worst) < LIMIT)
 
 
-def far_heads_again(first_head, refs, store):
+def far_heads_again(first_group, refs, store):
     wide_ref, near_kv, far_kv, first_ref, acc_ref, near_tile, far_tile = refs
-
-    @pl.loop(0, acc_ref.shape[1] // (2 * HEAD_DIM))
+    tokens_here = far_tile.shape[1]
+
+    @pl.loop(0, acc_ref.shape[0] // tokens_here)
     def _(local):
-        cols = lanes(first_head + local, 2 * HEAD_DIM)
-        query_rows = wide_ref[:, cols]
+        head = first_group * GROUP + local
+        rows = pl.ds(pl.multiple_of(head * tokens_here, tokens_here), tokens_here)
+        query_rows = wide_ref[rows, :]
         kv = local // GROUP
-        near_scores = scores_of(query_rows, key_of(near_kv, kv, near_tile))
-        far_scores = scores_of(query_rows, key_of(far_kv, kv, far_tile))
+        near_scores = product(query_rows, key_of(near_kv, kv, near_tile))
+        far_scores = product(query_rows, key_of(far_kv, kv, far_tile))
         top = jnp.max(jnp.maximum(near_scores, far_scores), axis=1, keepdims=True)
         top = jnp.maximum(top, 0.0)
         acc = (
-            first_ref[:, cols] * jnp.exp2(-top * SCALE)
-            + spread(mass_of(near_scores - top), value_of(near_kv, kv))
-            + spread(mass_of(far_scores - top), value_of(far_kv, kv))
+            first_ref[rows, :] * jnp.exp2(-top * SCALE)
+            + product(mass_of(near_scores - top), value_of(near_kv, kv))
+            + product(mass_of(far_scores - top), value_of(far_kv, kv))
         )
         store(local, (acc[:, :HEAD_DIM] / acc[:, HEAD_DIM:]).astype(jnp.bfloat16))
 
 
 def far_other_kernel(*refs):
     refs, out_ref = refs[:7], refs[7]
-    first_head = 0
 
     def store(local, block):
         out_ref[0, :, lanes(local, HEAD_DIM)] = block
 
-    too_high = far_heads(first_head, refs, store)
+    too_high = far_heads(0, refs, store)
 
     @pl.when(too_high)
     def _():
-        far_heads_again(first_head, refs, store)
+        far_heads_again(0, refs, store)
 
 
 def far_own_kernel(*refs):
@@ -325,7 +328,7 @@
     tokens_here = sent_ref.shape[1]
     heads_half = width // HEAD_DIM
     mp = lax.axis_index("mp")
-    first_head = heads_half
+    first_group = heads_half // GROUP
     sent_copy = pltpu.make_async_copy(
         sent_ref.at[0], out_ref.at[0, :, lanes(1 - mp, width)], sem.at[heads_half]
     )
@@ -363,7 +366,7 @@
         state["far"] = jnp.where(lane == local, far, state["far"])
         state["size"] = jnp.where(lane == local, size, state["size"])
 
-    too_high = far_heads(first_head, refs, store)
+    too_high = far_heads(first_group, refs, store)
     gap_ref[...] = gap_of(state["far"], state["size"])
     gap_copy.start()
     sent_copy.wait()
@@ -376,7 +379,7 @@
         def store_again(local, block):
             mine_ref[:, lanes(local, HEAD_DIM)] = block
 
-        far_heads_again(first_head, refs, store_again)
+        far_heads_again(first_group, refs, store_again)
         far = size = jnp.zeros((tokens_here, HEAD_DIM), jnp.float32)
         for local in range(heads_half):
             parts = squares(local, mine_ref[:, lanes(local, HEAD_DIM)])
@@ -418,7 +421,7 @@
     count = lax.axis_size("row")
     f32, bf16 = jnp.float32, jnp.bfloat16
     shape = jax.ShapeDtypeStruct
-    tile_type = shape((tokens_here, HEAD_DIM), bf16)
+    tile_type = shape((HEAD_DIM, tokens_here), bf16)
     work = 8 * heads_local * tokens_here * tokens_here * HEAD_DIM
 
     near_route = [(i - 1, i) for i in range(1, count)]
@@ -445,8 +448,8 @@
     wide, acc, near_tile, far_tile = call(
         diagonal_kernel,
         (
-            shape((tokens_here, 2 * width), bf16),
-            shape((tokens_here, 2 * width), f32),
+            shape((heads_local * tokens_here, 2 * HEAD_DIM), bf16),
+            shape((heads_local * tokens_here, 2 * HEAD_DIM), f32),
             tile_type,
             tile_type,
         ),
@@ -465,7 +468,7 @@
     def near(own, block):
         return call(
             lambda *refs: near_kernel(own, *refs),
-            shape((tokens_here, width), f32),
+            shape((heads_local // 2 * tokens_here, 2 * HEAD_DIM), f32),
             [VMEM] * 4,
             VMEM,
             work,

time: 44.7 us -> 44.4 us (level)
  the two profiles are of different devices: /device:TPU:16 before, /device:TPU:22 now
where the time goes in v4:
time: 44.4 us; the launch traced here: 44.2 us
  waiting for transfers between devices  19.1 us (43%)
  starting transfers between devices  14 us (32%)
  Pallas kernels  10.3 us (23%)
  between operations  0.71 us (2%)
    ppermute x1, waiting for transfers between devices, per_device_paired(): own_near = lax.ppermute(own, 'row', near_route)  7.1 us
    ppermute x1, waiting for transfers between devices, per_device_paired(): other_near = lax.ppermute(other, 'row', near_route)  6.45 us
    ppermute x1, waiting for transfers between devices, per_device_paired(): own_far = lax.ppermute(own_near, 'row', far_route)  5.23 us
    ppermute x1, starting transfers between devices, per_device_paired(): own_near = lax.ppermute(own, 'row', near_route)  3.49 us
    ppermute x1, starting transfers between devices, per_device_paired(): other_near = lax.ppermute(other, 'row', near_route)  3.48 us
    ppermute x1, starting transfers between devices, per_device_paired(): own_far = lax.ppermute(own_near, 'row', far_route)  3.47 us
    ppermute x1, starting transfers between devices, per_device_paired(): other_far = lax.ppermute(other_near, 'row', far_route)  3.47 us
    pallas_call x1, Pallas kernels, per_device_paired(): call(diagonal_kernel, (shape((heads_local * tokens_here, 2 * HEAD_DIM), b...  2.69 us
  transfers between devices with their start and end apart: 5, of which 4 were waited for; matrix products, arithmetic and copies ran while one was open for 0% of the time, Pallas kernels for 14%

profile of v4, /device:TPU:22, one launch (start us, length us, event | category | flops | bytes accessed | tf_op | source)
XLA Modules:
  0.0 44.2 jit_solution(10515752814670787077)
XLA Ops:
  0.6 1.0 %shard_map.59.after_ref.other_ref = bf16[2,256,256]{2,1,0:T(8,128)(2,1)S(1)} custom-call(bf16[1,256,512]{2,1,0:T(8,128)(2,1)} %k_hbm.3, bf16[1,256,512]{2,1,0:T(8,128)(2,1)} %v_hbm.3), custom_call_target="tpu_custom_call" | custom-call | flops 1342177280 | bytes 4194304 | tf_op jit(solution)/shard_map/pallas_call | solution.py:430
  1.6 3.5 %collective-permute-start.2 = (bf16[2,256,256]{2,1,0:T(8,128)(2,1)S(1)}, bf16[2,256,256]{2,1,0:T(8,128)(2,1)S(1)}, u32[]{:S(2)}, u32[]{:S(2)}) collective-permute-start(bf16[2,256,256]{2,1,0:T(8,128)(2,1)S(1)} %shard_map.59.after_ref.other_ref), channel_id=1, source_target_pairs={{0,4},{4,8},{8,12},{1,5},{5,9},{9,13},{2,6},{6,10},{10,14},{3,7},{... | collective-permute-start | bytes 786440 | tf_op jit(solution)/shard_map/ppermute | solution.py:438
  5.1 6.4 %collective-permute-done.2.refs_1_ = bf16[2,256,256]{2,1,0:T(8,128)(2,1)S(1)} collective-permute-done((bf16[2,256,256]{2,1,0:T(8,128)(2,1)S(1)}, bf16[2,256,256]{2,1,0:T(8,128)(2,1)S(1)}, u32[]{:S(2)}, u32[]{:S(2)}) %collective-permute-start.2) | collective-permute-done | bytes 262176 | tf_op jit(solution)/shard_map/ppermute | solution.py:438
  11.5 3.5 %collective-permute-start.3 = (bf16[2,256,256]{2,1,0:T(8,128)(2,1)S(1)}, bf16[2,256,256]{2,1,0:T(8,128)(2,1)S(1)}, u32[]{:S(2)}, u32[]{:S(2)}) collective-permute-start(bf16[2,256,256]{2,1,0:T(8,128)(2,1)S(1)} %collective-permute-done.2.refs_1_), channel_id=1, source_target_pairs={{4,8},{8,12},{5,9},{9,13},{6,10},{10,14},{7,11},{11,15},{20,24},{2... | collective-permute-start | bytes 786440 | tf_op jit(solution)/shard_map/ppermute | solution.py:466
  15.0 1.5 %shard_map.60 = (bf16[2,256,256]{2,1,0:T(8,128)(2,1)S(1)}, bf16[256,2560]{1,0:T(8,128)(2,1)S(1)}) custom-call(bf16[1,256,512]{2,1,0:T(8,128)(2,1)} %k_hbm.3, bf16[1,256,512]{2,1,0:T(8,128)(2,1)} %v_hbm.3, bf16[1,256,2560]{2,1,0:T(8,128)(2,1)} %q_hbm.1, bf16[2,256,256]{2,1,0:T(8,128)(2,1)S(1)} %shard_map.59.after_ref.other_ref), custom_call_target="tpu_custom_call" | custom-call | flops 1342177280 | bytes 4194304 | tf_op jit(solution)/shard_map/pallas_call | solution.py:439
  16.6 2.7 %shard_map.61 = (bf16[5120,256]{1,0:T(8,128)(2,1)S(1)}, f32[5120,256]{1,0:T(8,128)S(1)}, bf16[128,256]{1,0:T(8,128)(2,1)S(1)}, bf16[128,256]{1,0:T(8,128)(2,1)S(1)}) custom-call(s32[2]{0:T(128)} %len_hbm.1, bf16[256,2560]{1,0:T(8,128)(2,1)S(1)} %get-tuple-element.8.q_ref, bf16[2,256,256]{2,1,0:T(8,128)(2,1)S(1)} %shard_map.59.after_ref.other_ref, ...), custom_call_target="tpu_custom_call" | custom-call | flops 1342177280 | bytes 4194304 | tf_op jit(solution)/shard_map/pallas_call | solution.py:448
  19.3 1.0 %shard_map.63.refs_4_ = f32[2560,256]{1,0:T(8,128)S(1)} custom-call(bf16[5120,256]{1,0:T(8,128)(2,1)S(1)} %get-tuple-element.10.refs_0_, bf16[2,256,256]{2,1,0:T(8,128)(2,1)S(1)} %collective-permute-done.2.refs_1_, f32[5120,256]{1,0:T(8,128)S(1)} %get-tuple-element.11.refs_2_.refs_3_, bf16[128,256]{1,0:T(8,128)(2,1)S(1)} %get-tuple-element.12.refs_3_.refs_5_), custom_call_target="tpu_custom_call" | custom-call | flops 1342177280 | bytes 4194304 | tf_op jit(solution)/shard_map/pallas_call | solution.py:469
  20.3 0.3 collective-permute-done.3.refs_2_
  20.6 1.1 %shard_map.64.refs_7_ = bf16[1,256,1280]{2,1,0:T(8,128)(2,1)S(1)} custom-call(bf16[5120,256]{1,0:T(8,128)(2,1)S(1)} %get-tuple-element.10.refs_0_, bf16[2,256,256]{2,1,0:T(8,128)(2,1)S(1)} %collective-permute-done.2.refs_1_, bf16[2,256,256]{2,1,0:T(8,128)(2,1)S(1)} %collective-permute-done.3.refs_2_, f32[5120,256]{1,0:T(8,128)S(1)} %get-tuple-element.11.refs_2_.refs_3_, ...), custom_call_target="tpu_custom_call" | custom-call | flops 1342177280 | bytes 4194304 | tf_op jit(solution)/shard_map/pallas_call | solution.py:480
  21.7 0.1 collective-permute-start.4
  21.8 3.5 %collective-permute-start = (bf16[2,256,256]{2,1,0:T(8,128)(2,1)S(1)}, bf16[2,256,256]{2,1,0:T(8,128)(2,1)S(1)}, u32[]{:S(2)}, u32[]{:S(2)}) collective-permute-start(bf16[2,256,256]{2,1,0:T(8,128)(2,1)S(1)} %get-tuple-element.9.own_ref), channel_id=1, source_target_pairs={{0,4},{4,8},{8,12},{1,5},{5,9},{9,13},{2,6},{6,10},{10,14},{3,7},{... | collective-permute-start | bytes 786440 | tf_op jit(solution)/shard_map/ppermute | solution.py:447
  25.3 7.1 %collective-permute-done.refs_1_ = bf16[2,256,256]{2,1,0:T(8,128)(2,1)S(1)} collective-permute-done((bf16[2,256,256]{2,1,0:T(8,128)(2,1)S(1)}, bf16[2,256,256]{2,1,0:T(8,128)(2,1)S(1)}, u32[]{:S(2)}, u32[]{:S(2)}) %collective-permute-start) | collective-permute-done | bytes 262176 | tf_op jit(solution)/shard_map/ppermute | solution.py:447
  32.4 3.5 %collective-permute-start.1 = (bf16[2,256,256]{2,1,0:T(8,128)(2,1)S(1)}, bf16[2,256,256]{2,1,0:T(8,128)(2,1)S(1)}, u32[]{:S(2)}, u32[]{:S(2)}) collective-permute-start(bf16[2,256,256]{2,1,0:T(8,128)(2,1)S(1)} %collective-permute-done.refs_1_), channel_id=1, source_target_pairs={{4,8},{8,12},{5,9},{9,13},{6,10},{10,14},{7,11},{11,15},{20,24},{2... | collective-permute-start | bytes 786440 | tf_op jit(solution)/shard_map/ppermute | solution.py:478
  35.9 1.0 %shard_map.62.refs_4_ = f32[2560,256]{1,0:T(8,128)S(1)} custom-call(bf16[5120,256]{1,0:T(8,128)(2,1)S(1)} %get-tuple-element.10.refs_0_, bf16[2,256,256]{2,1,0:T(8,128)(2,1)S(1)} %collective-permute-done.refs_1_, f32[5120,256]{1,0:T(8,128)S(1)} %get-tuple-element.11.refs_2_.refs_3_, bf16[128,256]{1,0:T(8,128)(2,1)S(1)} %get-tuple-element.12.refs_3_.refs_5_), custom_call_target="tpu_custom_call" | custom-call | flops 1342177280 | bytes 4194304 | tf_op jit(solution)/shard_map/pallas_call | solution.py:469
  36.9 5.2 %collective-permute-done.1.refs_2_ = bf16[2,256,256]{2,1,0:T(8,128)(2,1)S(1)} collective-permute-done((bf16[2,256,256]{2,1,0:T(8,128)(2,1)S(1)}, bf16[2,256,256]{2,1,0:T(8,128)(2,1)S(1)}, u32[]{:S(2)}, u32[]{:S(2)}) %collective-permute-start.1) | collective-permute-done | bytes 262176 | tf_op jit(solution)/shard_map/ppermute | solution.py:478
  42.1 0.0 collective-permute-done.4.refs_8_
  42.1 2.0 %shard_map.65 = (bf16[1,256,2560]{2,1,0:T(8,128)(2,1)}, f32[10,256]{1,0:T(8,128)}) custom-call(bf16[5120,256]{1,0:T(8,128)(2,1)S(1)} %get-tuple-element.10.refs_0_, bf16[2,256,256]{2,1,0:T(8,128)(2,1)S(1)} %collective-permute-done.refs_1_, bf16[2,256,256]{2,1,0:T(8,128)(2,1)S(1)} %collective-permute-done.1.refs_2_, ...), custom_call_target="tpu_custom_call" | custom-call | flops 1342177280 | bytes 4194304 | tf_op jit(solution)/shard_map/pallas_call | solution.py:484
Async XLA Ops:
  1.6 9.9 %collective-permute-start.2 = (bf16[2,256,256]{2,1,0:T(8,128)(2,1)S(1)}, bf16[2,256,256]{2,1,0:T(8,128)(2,1)S(1)}, u32[]{:S(2)}, u32[]{:S(2)}) collective-permute-start(bf16[2,256,256]{2,1,0:T(8,128)(2,1)S(1)} %shard_map.59.after_ref.other_ref), channel_id=1, source_target_pairs={{0,4},{4,8},{8,12},{1,5},{5,9},{9,13},{2,6},{6,10},{10,14},{3,7},{... | collective-permute-start | bytes 786440 | tf_op jit(solution)/shard_map/ppermute | solution.py:438
  11.5 9.1 %collective-permute-start.3 = (bf16[2,256,256]{2,1,0:T(8,128)(2,1)S(1)}, bf16[2,256,256]{2,1,0:T(8,128)(2,1)S(1)}, u32[]{:S(2)}, u32[]{:S(2)}) collective-permute-start(bf16[2,256,256]{2,1,0:T(8,128)(2,1)S(1)} %collective-permute-done.2.refs_1_), channel_id=1, source_target_pairs={{4,8},{8,12},{5,9},{9,13},{6,10},{10,14},{7,11},{11,15},{20,24},{2... | collective-permute-start | bytes 786440 | tf_op jit(solution)/shard_map/ppermute | solution.py:466
  21.7 20.4 %collective-permute-start.4 = (bf16[1,256,1280]{2,1,0:T(8,128)(2,1)S(1)}, bf16[1,256,1280]{2,1,0:T(8,128)(2,1)S(1)}, u32[]{:S(2)}, u32[]{:S(2)}) collective-permute-start(bf16[1,256,1280]{2,1,0:T(8,128)(2,1)S(1)} %shard_map.64.refs_7_), channel_id=1, source_target_pairs={{0,1},{1,0},{2,3},{3,2},{4,5},{5,4},{6,7},{7,6},{8,9},{9,8},{10,11... | collective-permute-start | bytes 1966088 | tf_op jit(solution)/shard_map/ppermute | solution.py:483
  21.8 10.6 %collective-permute-start = (bf16[2,256,256]{2,1,0:T(8,128)(2,1)S(1)}, bf16[2,256,256]{2,1,0:T(8,128)(2,1)S(1)}, u32[]{:S(2)}, u32[]{:S(2)}) collective-permute-start(bf16[2,256,256]{2,1,0:T(8,128)(2,1)S(1)} %get-tuple-element.9.own_ref), channel_id=1, source_target_pairs={{0,4},{4,8},{8,12},{1,5},{5,9},{9,13},{2,6},{6,10},{10,14},{3,7},{... | collective-permute-start | bytes 786440 | tf_op jit(solution)/shard_map/ppermute | solution.py:447
  32.4 9.7 %collective-permute-start.1 = (bf16[2,256,256]{2,1,0:T(8,128)(2,1)S(1)}, bf16[2,256,256]{2,1,0:T(8,128)(2,1)S(1)}, u32[]{:S(2)}, u32[]{:S(2)}) collective-permute-start(bf16[2,256,256]{2,1,0:T(8,128)(2,1)S(1)} %collective-permute-done.refs_1_), channel_id=1, source_target_pairs={{4,8},{8,12},{5,9},{9,13},{6,10},{10,14},{7,11},{11,15},{20,24},{2... | collective-permute-start | bytes 786440 | tf_op jit(solution)/shard_map/ppermute | solution.py:478
